TPU v7x, 32 devices: a whole 2x2x4 slice. The times are simulated.
32 devices in a mesh: gx: 4 (over y, x), gy: 8 (over z, core).
Axes of the slice: x: 2, y: 2, z: 4, core: 2. Of those that a mesh axis runs over, the one named last changes fastest.
Arguments:
- point_coords: float32 [128, 3, 256], P(('gx', 'gy')), may hold values from -2 to 2
- charge: float32 [128, 256], P(('gx', 'gy')), may hold values from -0.12 to 0.12
- shell_index: int32 [128, 32, 256], P(('gx', 'gy')), may hold values from 0 to 63
- neighbours: int32 [128, 32], P(('gx', 'gy')), may hold values from 0 to 1023, as said below
- neighbour_count: int32 [128], P(('gx', 'gy')), may hold values from 24 to 32
- batch_load: int32 [32], P(('gx', 'gy')), may hold values from 3 to 4, as said below
- atom_coords: float32 [3, 1024], replicated, may hold values from -2 to 2
- owner_slot: int32 [1024], replicated, may hold values from 0 to 1023, as said below
Outputs:
- potential: float32 [128, 256], P(('gx', 'gy'))
- moments: float32 [1024, 3136], P(('gx', 'gy'))
Inputs may be any that keep to these rules, and one draw needn't show every extreme that they name: `neighbours`: atom labels. On every device, at most 4 of its 128 neighbour slots, live or not, name atoms whose owner_slot lies in one block of 32 rows; on every device some block gets exactly 4. `owner_slot`: each row number once. `batch_load`: some device has all 4 slots live.
All inputs are finite; a program needn't handle non-finite values.
Results may differ from a plain program's by a relative error of at most 0.0003.
Values sent between devices are 32-bit elements; how exact they have to be, the bound alone decides.
No kernel may reach another device: no remote copies, remote signals or barrier semaphores. Data moves between devices by JAX's collectives and lax.ppermute only.
A program may use at most 64 MiB of HBM per device.

v0:
```python
import math

import jax
import jax.numpy as jnp
from jax import lax
from jax.sharding import PartitionSpec as P

SHELLS = 64


SOFTEN = 0.01
HIGHEST = lax.Precision.HIGHEST


def harmonics(along_x, along_y, along_z):
    cosines = [jnp.ones_like(along_x)]
    sines = [jnp.zeros_like(along_x)]
    for azimuth in range(1, 7):
        previous_cos = cosines[-1]
        previous_sin = sines[-1]
        cosines.append(previous_cos * along_x - previous_sin * along_y)
        sines.append(previous_cos * along_y + previous_sin * along_x)
    legendre = {}
    for azimuth in range(7):
        legendre[azimuth, azimuth] = jnp.ones_like(along_z) * float(
            math.prod(range(1, 2 * azimuth, 2))
        )
        if azimuth < 6:
            legendre[azimuth + 1, azimuth] = (
                (2 * azimuth + 1) * along_z * legendre[azimuth, azimuth]
            )
        for degree in range(azimuth + 2, 7):
            legendre[degree, azimuth] = (
                (2 * degree - 1) * along_z * legendre[degree - 1, azimuth]
                - (degree + azimuth - 1) * legendre[degree - 2, azimuth]
            ) / (degree - azimuth)
    results = []
    for degree in range(7):
        for signed in range(-degree, degree + 1):
            azimuth = abs(signed)
            factor = math.sqrt(
                (2 * degree + 1)
                / (4 * math.pi)
                * math.factorial(degree - azimuth)
                / math.factorial(degree + azimuth)
            )
            if signed == 0:
                results.append(factor * legendre[degree, 0])
            elif signed > 0:
                results.append(
                    math.sqrt(2.0) * factor * legendre[degree, azimuth] * cosines[azimuth]
                )
            else:
                results.append(math.sqrt(2.0) * factor * legendre[degree, azimuth] * sines[azimuth])
    return jnp.stack(results)


def green_table():
    shell_rank = jnp.arange(SHELLS, dtype=jnp.float32)
    radius = 0.5 * jnp.exp(2.3 * shell_rank / SHELLS)
    nearer = jnp.minimum(radius[:, None], radius[None, :])
    farther = jnp.maximum(radius[:, None], radius[None, :])
    kernels = []
    for degree in range(7):
        kernel = 4.0 * math.pi / (2 * degree + 1) * nearer**degree / farther ** (degree + 1)
        kernels.extend([kernel] * (2 * degree + 1))
    return jnp.stack(kernels)


def batch_geometry(coords, atom_place, count):
    offset = coords[:, None, :] - atom_place[:, :, None]
    squared = jnp.sum(offset * offset, axis=0)
    scale = 1.0 / jnp.sqrt(squared + SOFTEN)
    harmonic = harmonics(offset[0] * scale, offset[1] * scale, offset[2] * scale)
    slot_live = jnp.arange(atom_place.shape[1], dtype=jnp.int32) < count
    closeness = jnp.where(slot_live[:, None], 1.0 / (1.0 + squared), 0.0)
    share = closeness / jnp.sum(closeness, axis=0, keepdims=True)
    return (harmonic, share)


def body(
    point_coords,
    charge,
    shell_index,
    neighbours,
    neighbour_count,
    batch_load,
    atom_coords,
    owner_slot,
):
    batches = charge.shape[0]
    slots = neighbours.shape[1]
    count_gx = lax.axis_size("gx")
    count_gy = lax.axis_size("gy")
    devices = count_gx * count_gy
    owned = owner_slot.shape[0] // devices
    spaces = batches * slots
    per_peer = spaces // devices
    slot_rank = jnp.arange(slots, dtype=jnp.int32)
    shell_rank = jnp.arange(SHELLS, dtype=jnp.int32)
    live_batch = (jnp.arange(batches, dtype=jnp.int32) < batch_load[0]).astype(jnp.float32)
    green = green_table()

    def forward(inputs):
        coords, weights_here, shells_here, labels, count, live = inputs
        harmonic, share = batch_geometry(coords, atom_coords[:, labels], count)
        weighted = harmonic * (share * weights_here[None, :] * live)[None]
        selector = (shells_here[:, :, None] == shell_rank).astype(jnp.float32)
        partial_value = jnp.einsum("lip,ips->ils", weighted, selector, precision=HIGHEST)
        return (partial_value, harmonic)

    partial_value, harmonic = lax.map(
        forward, (point_coords, charge, shell_index, neighbours, neighbour_count, live_batch)
    )
    width = partial_value.shape[2] * partial_value.shape[3]
    rows_flat = partial_value.reshape(batches * slots, width)
    target_slot = owner_slot[neighbours.reshape(-1)]
    owner = target_slot // owned
    local = target_slot % owned
    row_live = (
        (slot_rank[None, :] < neighbour_count[:, None]) & (live_batch[:, None] > 0.0)
    ).reshape(-1)
    marks = (
        (owner[:, None] == jnp.arange(devices, dtype=jnp.int32)[None, :]) & row_live[:, None]
    ).astype(jnp.int32)
    before = jnp.cumsum(marks, axis=0) - marks
    place = jnp.sum(before * marks, axis=1)
    target = jnp.where(row_live, owner * per_peer + place, spaces)
    outgoing = jnp.zeros((spaces, width), jnp.float32).at[target].set(rows_flat, mode="drop")
    labels_out = (
        jnp.zeros((spaces,), jnp.float32).at[target].set(local.astype(jnp.float32), mode="drop")
    )
    arrived, arrived_label = (
        lax.all_to_all(outgoing, ("gx", "gy"), split_axis=0, concat_axis=0, tiled=True),
        lax.all_to_all(labels_out, ("gx", "gy"), split_axis=0, concat_axis=0, tiled=True),
    )
    picker = (jnp.arange(owned, dtype=jnp.float32)[:, None] == arrived_label[None, :]).astype(
        jnp.float32
    )
    moments = jnp.dot(picker, arrived, precision=HIGHEST, preferred_element_type=jnp.float32)
    arrived_rows = arrived_label.astype(jnp.int32)
    tables = jnp.einsum(
        "lst,alt->als", green, moments.reshape(owned, -1, SHELLS), precision=HIGHEST
    )
    reply = tables.reshape(owned, width)[arrived_rows]
    returned = lax.all_to_all(reply, ("gx", "gy"), split_axis=0, concat_axis=0, tiled=True)
    fetched = returned[jnp.minimum(target, spaces - 1)].reshape(batches, slots, -1, SHELLS)

    def evaluate(inputs):
        table_rows, harmonic_here, shells_here, count, live = inputs
        selector = (shells_here[:, :, None] == shell_rank).astype(jnp.float32)
        picked = jnp.einsum("jls,jps->jlp", table_rows, selector, precision=HIGHEST)
        total = jnp.sum(picked * jnp.transpose(harmonic_here, (1, 0, 2)), axis=1)
        slot_live = slot_rank < count
        return jnp.sum(jnp.where(slot_live[:, None], total, 0.0), axis=0) * live

    potential = lax.map(evaluate, (fetched, harmonic, shell_index, neighbour_count, live_batch))
    return (potential, moments)


def solution(mesh):
    return jax.shard_map(
        body,
        mesh=mesh,
        in_specs=(
            P(("gx", "gy"), None, None),
            P(("gx", "gy"), None),
            P(("gx", "gy"), None, None),
            P(("gx", "gy"), None),
            P(("gx", "gy")),
            P(("gx", "gy")),
            P(),
            P(),
        ),
        out_specs=(P(("gx", "gy"), None), P(("gx", "gy"), None)),
        check_vma=False,
    )
```

profile of v0, /device:TPU:0, one launch (start us, length us, event | category | flops | bytes accessed | tf_op | source)
XLA Modules:
  0.0 206.6 jit_solution(7153771398517581746)
XLA Ops:
  6.3 7.3 %all-to-all-start = ((f32[32,4,1]{1,2,0:T(1,128)}), f32[32,4,1]{1,2,0:T(1,128)S(1)}, u32[]{:S(2)}, u32[]{:S(2)}) async-start(f32[32,4,1]{1,2,0:T(1,128)} %bitcast.5), calls=%async_computation | async-start | bytes 32768 | tf_op jit(solution)/shard_map/all_to_all | solution.py:135
  17.2 44.3 %while.28 = (s32[]{:T(128)}, f32[4,32,49,64]{3,2,1,0:T(8,128)}, f32[4,49,32,256]{3,2,1,0:T(8,128)}, f32[4,3,256]{2,0,1:T(4,128)}, s32[4,32]{1,0:T(4,128)}, /*ind...) while((s32[]{:T(128)}, f32[4,32,49,64]{3,2,1,0:T(8,128)}, ...), condition=%wide.region_6.7_spmd.clone, body=%wide.region_3.6_spmd.clone.sunk | while | flops 312320896 | bytes 15036029 | solution.py:112
  20.5 1.3 bitcast_dynamic-update-slice_fusion.2
  25.3 2.9 %fusion.71 = f32[4,32,49,64]{3,2,1,0:T(8,128)} fusion(f32[4,32,49,64]{3,2,1,0:T(8,128)} %get-tuple-element.636, s32[]{:T(128)} %get-tuple-element.635, f32[49,32,256]{2,1,0:T(8,128)S(1)} %broadcast_multiply_fusion.4, s32[32,256]{1,0:T(8,128)S(1)} %dynamic-slice_bitcast_fusion.4), kind=kOutput, calls=%fused_computation.14.clone.1 | convolution fusion | flops 308805632 | bytes 2556416 | tf_op jit(solution)/shard_map/while/body/eval_jaxpr/lip,ips->ils/dot_general | solution.py:109
  36.4 2.9 %fusion.71 = f32[4,32,49,64]{3,2,1,0:T(8,128)} fusion(f32[4,32,49,64]{3,2,1,0:T(8,128)} %get-tuple-element.636, s32[]{:T(128)} %get-tuple-element.635, f32[49,32,256]{2,1,0:T(8,128)S(1)} %broadcast_multiply_fusion.4, s32[32,256]{1,0:T(8,128)S(1)} %dynamic-slice_bitcast_fusion.4), kind=kOutput, calls=%fused_computation.14.clone.1 | convolution fusion | flops 308805632 | bytes 2556416 | tf_op jit(solution)/shard_map/while/body/eval_jaxpr/lip,ips->ils/dot_general | solution.py:109
  42.6 1.3 bitcast_dynamic-update-slice_fusion.2
  47.5 3.0 %fusion.71 = f32[4,32,49,64]{3,2,1,0:T(8,128)} fusion(f32[4,32,49,64]{3,2,1,0:T(8,128)} %get-tuple-element.636, s32[]{:T(128)} %get-tuple-element.635, f32[49,32,256]{2,1,0:T(8,128)S(1)} %broadcast_multiply_fusion.4, s32[32,256]{1,0:T(8,128)S(1)} %dynamic-slice_bitcast_fusion.4), kind=kOutput, calls=%fused_computation.14.clone.1 | convolution fusion | flops 308805632 | bytes 2556416 | tf_op jit(solution)/shard_map/while/body/eval_jaxpr/lip,ips->ils/dot_general | solution.py:109
  53.7 1.3 bitcast_dynamic-update-slice_fusion.2
  58.6 2.9 %fusion.71 = f32[4,32,49,64]{3,2,1,0:T(8,128)} fusion(f32[4,32,49,64]{3,2,1,0:T(8,128)} %get-tuple-element.636, s32[]{:T(128)} %get-tuple-element.635, f32[49,32,256]{2,1,0:T(8,128)S(1)} %broadcast_multiply_fusion.4, s32[32,256]{1,0:T(8,128)S(1)} %dynamic-slice_bitcast_fusion.4), kind=kOutput, calls=%fused_computation.14.clone.1 | convolution fusion | flops 308805632 | bytes 2556416 | tf_op jit(solution)/shard_map/while/body/eval_jaxpr/lip,ips->ils/dot_general | solution.py:109
  61.6 3.9 %reshape.1138 = f32[128,3136]{1,0:T(8,128)} reshape(f32[4,32,49,64]{3,2,1,0:T(8,128)} %get-tuple-element.303) | data formatting | bytes 3211264 | tf_op jit(solution)/shard_map/reshape | solution.py:116
  65.5 2.8 %scatter_custom_fusion.1 = f32[128,3136]{1,0:T(8,128)S(1)} fusion(s32[128]{0:T(128)S(1)} %fusion.53, f32[128,3136]{1,0:T(8,128)} %reshape.1138, f32[]{:T(128)} %constant.487.clone.1), kind=kCustom, calls=%fused_computation.126 | custom fusion | bytes 1606144 | tf_op jit(solution)/shard_map/scatter | solution.py:129
  68.3 1.6 all_to_all.24
  70.0 6.0 %all-to-all-start.1 = ((f32[32,4,3136]{2,1,0:T(4,128)}), f32[32,4,3136]{2,1,0:T(4,128)S(1)}, u32[]{:S(2)}, u32[]{:S(2)}) async-start(f32[32,4,3136]{2,1,0:T(4,128)} %all_to_all.24), calls=%async_computation.1 | async-start | bytes 3276800 | tf_op jit(solution)/shard_map/all_to_all | solution.py:134
  78.7 37.3 %all-to-all-done.1 = f32[32,4,3136]{2,1,0:T(4,128)S(1)} async-done(((f32[32,4,3136]{2,1,0:T(4,128)}), f32[32,4,3136]{2,1,0:T(4,128)S(1)}, u32[]{:S(2)}, u32[]{:S(2)}) %all-to-all-start.1) | async-done | bytes 1605664 | tf_op jit(solution)/shard_map/all_to_all | solution.py:134
  117.5 4.0 %convolution_bitcast_fusion = f32[32,49,64]{2,0,1:T(8,128)S(1)} fusion(f32[49,64,64]{2,1,0:T(8,128)} %copy-done.1, f32[32,49,64]{2,1,0:T(8,128)S(1)} %reshape.1091), kind=kOutput, calls=%fused_computation.125 | convolution fusion | flops 77070336 | bytes 1605632 | tf_op jit(solution)/shard_map/lst,alt->als/dot_general | solution.py:142
  123.4 1.6 all_to_all.27
  125.1 2.7 %all-to-all-start.2 = ((f32[32,4,3136]{2,1,0:T(4,128)}), f32[32,4,3136]{2,1,0:T(4,128)S(1)}, u32[]{:S(2)}, u32[]{:S(2)}) async-start(f32[32,4,3136]{2,1,0:T(4,128)} %all_to_all.27), calls=%async_computation.2 | async-start | bytes 3276800 | tf_op jit(solution)/shard_map/all_to_all | solution.py:146
  127.8 40.1 %all-to-all-done.2 = f32[32,4,3136]{2,1,0:T(4,128)S(1)} async-done(((f32[32,4,3136]{2,1,0:T(4,128)}), f32[32,4,3136]{2,1,0:T(4,128)S(1)}, u32[]{:S(2)}, u32[]{:S(2)}) %all-to-all-start.2) | async-done | bytes 1605664 | tf_op jit(solution)/shard_map/all_to_all | solution.py:146
  169.8 2.2 %reshape.1093 = f32[4,32,49,64]{3,2,1,0:T(8,128)} reshape(f32[128,3136]{1,0:T(8,128)S(1)} %gather_fusion.3) | data formatting | bytes 3211264 | tf_op jit(solution)/shard_map/reshape | solution.py:147
  172.0 34.6 %while.29 = (s32[]{:T(128)}, f32[4,256]{1,0:T(4,128)}, s32[4]{0:T(128)S(1)}, f32[4,32,49,64]{3,2,1,0:T(8,128)}, s32[4,32,256]{2,1,0:T(8,128)S(1)}, /*index=5*/f3...) while((s32[]{:T(128)}, f32[4,256]{1,0:T(4,128)}, s32[4]{0:T(128)S(1)}, ...), condition=%wide.region_11.12_spmd.clone, body=%wide.region_8.11_spmd.clone.sunk | while | flops 309616672 | bytes 5904073 | solution.py:157
  172.0 1.5 constant_dynamic-slice_fusion.9
  173.5 3.3 %fusion.73 = f32[32,256]{1,0:T(8,128)S(1)} fusion(f32[1,49,32,256]{3,2,1,0:T(8,128)S(1)} %constant_dynamic-slice_fusion.9, s32[32,256]{1,0:T(8,128)S(1)} %dynamic-slice_bitcast_fusion.5, f32[4,32,49,64]{3,2,1,0:T(8,128)} %get-tuple-element.678, s32[]{:T(128)} %get-tuple-element.666), kind=kOutput, calls=%fused_computation.115.clone.1 | convolution fusion | flops 309600256 | bytes 2589184 | tf_op jit(solution)/shard_map/while/body/eval_jaxpr/jls,jps->jlp/dot_general | solution.py:152
  179.3 1.3 dynamic_update_slice.34
  180.6 1.5 constant_dynamic-slice_fusion.9
  182.2 3.3 %fusion.73 = f32[32,256]{1,0:T(8,128)S(1)} fusion(f32[1,49,32,256]{3,2,1,0:T(8,128)S(1)} %constant_dynamic-slice_fusion.9, s32[32,256]{1,0:T(8,128)S(1)} %dynamic-slice_bitcast_fusion.5, f32[4,32,49,64]{3,2,1,0:T(8,128)} %get-tuple-element.678, s32[]{:T(128)} %get-tuple-element.666), kind=kOutput, calls=%fused_computation.115.clone.1 | convolution fusion | flops 309600256 | bytes 2589184 | tf_op jit(solution)/shard_map/while/body/eval_jaxpr/jls,jps->jlp/dot_general | solution.py:152
  188.0 1.3 dynamic_update_slice.34
  189.3 1.5 constant_dynamic-slice_fusion.9
  190.8 3.3 %fusion.73 = f32[32,256]{1,0:T(8,128)S(1)} fusion(f32[1,49,32,256]{3,2,1,0:T(8,128)S(1)} %constant_dynamic-slice_fusion.9, s32[32,256]{1,0:T(8,128)S(1)} %dynamic-slice_bitcast_fusion.5, f32[4,32,49,64]{3,2,1,0:T(8,128)} %get-tuple-element.678, s32[]{:T(128)} %get-tuple-element.666), kind=kOutput, calls=%fused_computation.115.clone.1 | convolution fusion | flops 309600256 | bytes 2589184 | tf_op jit(solution)/shard_map/while/body/eval_jaxpr/jls,jps->jlp/dot_general | solution.py:152
  196.7 1.3 dynamic_update_slice.34
  198.0 1.5 constant_dynamic-slice_fusion.9
  199.5 3.3 %fusion.73 = f32[32,256]{1,0:T(8,128)S(1)} fusion(f32[1,49,32,256]{3,2,1,0:T(8,128)S(1)} %constant_dynamic-slice_fusion.9, s32[32,256]{1,0:T(8,128)S(1)} %dynamic-slice_bitcast_fusion.5, f32[4,32,49,64]{3,2,1,0:T(8,128)} %get-tuple-element.678, s32[]{:T(128)} %get-tuple-element.666), kind=kOutput, calls=%fused_computation.115.clone.1 | convolution fusion | flops 309600256 | bytes 2589184 | tf_op jit(solution)/shard_map/while/body/eval_jaxpr/jls,jps->jlp/dot_general | solution.py:152
  205.3 1.3 dynamic_update_slice.34
  (380 shorter events, 53.3 us)
Async XLA Ops:
  0.6 2.4 %copy-start = (s32[1024]{0:T(1024)S(1)}, s32[1024]{0:T(1024)}, u32[]{:S(2)}) copy-start(s32[1024]{0:T(1024)} %param.19) | copy-start | bytes 12292
  0.6 16.5 %copy-start.5 = (s32[4]{0:T(128)S(1)}, s32[4]{0:T(128)}, u32[]{:S(2)}) copy-start(s32[4]{0:T(128)} %param.16) | copy-start | bytes 52
  0.7 16.3 %copy-start.4 = (f32[3,1024]{1,0:T(4,128)S(1)}, f32[3,1024]{1,0:T(4,128)}, u32[]{:S(2)}) copy-start(f32[3,1024]{1,0:T(4,128)} %param.18) | copy-start | bytes 36868
  0.7 16.5 %copy-start.3 = (s32[4,32,256]{2,1,0:T(8,128)S(1)}, s32[4,32,256]{2,1,0:T(8,128)}, u32[]{:S(2)}) copy-start(s32[4,32,256]{2,1,0:T(8,128)} %param.14) | copy-start | bytes 393220
  6.3 63.7 %all-to-all-start = ((f32[32,4,1]{1,2,0:T(1,128)}), f32[32,4,1]{1,2,0:T(1,128)S(1)}, u32[]{:S(2)}, u32[]{:S(2)}) async-start(f32[32,4,1]{1,2,0:T(1,128)} %bitcast.5), calls=%async_computation | async-start | bytes 32768 | tf_op jit(solution)/shard_map/all_to_all | solution.py:135
  70.0 46.0 %all-to-all-start.1 = ((f32[32,4,3136]{2,1,0:T(4,128)}), f32[32,4,3136]{2,1,0:T(4,128)S(1)}, u32[]{:S(2)}, u32[]{:S(2)}) async-start(f32[32,4,3136]{2,1,0:T(4,128)} %all_to_all.24), calls=%async_computation.1 | async-start | bytes 3276800 | tf_op jit(solution)/shard_map/all_to_all | solution.py:134
  77.1 1.6 copy-start.1
  117.3 4.2 %copy-start.2 = (f32[32,3136]{1,0:T(8,128)}, f32[32,3136]{1,0:T(8,128)S(1)}, u32[]{:S(2)}) copy-start(f32[32,3136]{1,0:T(8,128)S(1)} %fusion.48) | copy-start | bytes 1204228
  125.1 42.9 %all-to-all-start.2 = ((f32[32,4,3136]{2,1,0:T(4,128)}), f32[32,4,3136]{2,1,0:T(4,128)S(1)}, u32[]{:S(2)}, u32[]{:S(2)}) async-start(f32[32,4,3136]{2,1,0:T(4,128)} %all_to_all.27), calls=%async_computation.2 | async-start | bytes 3276800 | tf_op jit(solution)/shard_map/all_to_all | solution.py:146
where the time goes:
time: 208 us; the launch traced here: 207 us
  waiting for transfers between devices  77.4 us (37%)
  local copies, waits for them, and re-layouts  55.9 us (27%)
  matrix products  29.5 us (14%)
  other arithmetic  24.1 us (12%)
  starting transfers between devices  16 us (8%)
    all_to_all x1, waiting for transfers between devices, body(): lax.all_to_all(reply, ('gx', 'gy'), split_axis=0, concat_axis=0, tiled=True)  40.1 us
    all_to_all x1, waiting for transfers between devices, body(): lax.all_to_all(outgoing, ('gx', 'gy'), split_axis=0, concat_axis=0, tiled...  37.3 us
    dynamic_slice x28, local copies, waits for them, and re-layouts, body(): lax.map(forward, (point_coords, charge, shell_index, neighbours, neighbou...  15.4 us
    dot_general x4, matrix products, evaluate(): picked = jnp.einsum('jls,jps->jlp', table_rows, selector, precision=HIGHEST)  13 us
    dot_general x4, matrix products, forward(): jnp.einsum('lip,ips->ils', weighted, selector, precision=HIGHEST)  11.7 us
    all_to_all x1, starting transfers between devices, body(): lax.all_to_all(labels_out, ('gx', 'gy'), split_axis=0, concat_axis=0, til...  7.33 us
    dynamic_slice x4, local copies, waits for them, and re-layouts, body(): lax.map(evaluate, (fetched, harmonic, shell_index, neighbour_count, live_...  6.09 us
    all_to_all x1, starting transfers between devices, body(): lax.all_to_all(outgoing, ('gx', 'gy'), split_axis=0, concat_axis=0, tiled...  6.01 us
  transfers between devices with their start and end apart: 3, of which 2 were waited for; matrix products, arithmetic and copies ran while one was open for 27% of the time, Pallas kernels for 0%

commit v1 on v0

v1 whole, which is shorter than its diff:
```python
import functools
import math

import jax
import jax.numpy as jnp
from jax import lax
from jax.experimental import pallas as pl
from jax.experimental.pallas import tpu as pltpu
from jax.sharding import PartitionSpec as P

SHELLS = 64
LMAX = 6
HARM = (LMAX + 1) ** 2
PAD = 56
SOFTEN = 0.01
LANES = 128
FIELDS = 8
VMEM = pl.BlockSpec(memory_space=pltpu.VMEM)
SMEM = pl.BlockSpec(memory_space=pltpu.SMEM)
F32 = jnp.float32
BF16 = jnp.bfloat16


def iota(shape, axis):
    return lax.broadcasted_iota(jnp.int32, shape, axis)


def three_parts(value):
    first = value.astype(BF16)
    rest = value - first.astype(F32)
    second = rest.astype(BF16)
    third = (rest - second.astype(F32)).astype(BF16)
    return first, second, third


def pack_kernel(
    devices, count_ref, load_ref, label_ref, coord_ref, charge_ref, shell_ref, atom_ref, slot_ref, out_ref, table_ref
):
    batches, slots = label_ref.shape
    rows = batches * slots
    atoms = atom_ref.shape[1]
    owned = atoms // devices
    per_peer = rows // devices
    halves = charge_ref.shape[1] // LANES
    stride = out_ref.shape[0] // devices

    table_ref[...] = jnp.zeros_like(table_ref)
    table_ref[0:3, :] = atom_ref[...]
    for tile in range(atoms // LANES):
        table_ref[3:4, tile * LANES : (tile + 1) * LANES] = slot_ref[tile : tile + 1, :].astype(F32)
    label = jnp.concatenate([label_ref[b : b + 1, :] for b in range(batches)], axis=1)
    label = jnp.broadcast_to(label, (8, rows))
    high = lax.shift_right_logical(label, 7)
    low = lax.bitwise_and(label, 127)
    found = jnp.zeros((8, rows), F32)
    for tile in range(atoms // LANES):
        piece = table_ref[:, tile * LANES : (tile + 1) * LANES]
        picked = jnp.take_along_axis(piece, low, axis=1, mode="promise_in_bounds")
        found = jnp.where(high == tile, picked, found)
    slot = found[3:4, :]
    owner = jnp.floor((slot + 0.5) * (1.0 / owned))
    local = slot - owner * owned

    lane = iota((1, rows), 1)
    batch_row = jnp.zeros((1, rows), F32)
    live_row = jnp.zeros((1, rows), F32)
    for b in range(batches):
        inside = (lane >= b * slots) & (lane < (b + 1) * slots)
        batch_row = jnp.where(inside, float(b), batch_row)
        alive = inside & (lane - b * slots < count_ref[b]) & (load_ref[0] > b)
        live_row = jnp.where(alive, 1.0, live_row)
    sub = iota((8, rows), 0)
    fields = found
    for place, value in ((3, local), (4, batch_row), (5, live_row), (6, owner)):
        fields = jnp.where(sub == place, jnp.broadcast_to(value, (8, rows)), fields)
    columns = jnp.concatenate([fields, jnp.zeros((LANES - 8, rows), F32)], axis=0).T

    owner_column = columns[:, 6:7]
    earlier = (owner_column == owner) & (iota((rows, rows), 0) < iota((rows, rows), 1))
    rank = jnp.sum(earlier.astype(F32), axis=0, keepdims=True)
    target = (rank * devices + owner).astype(jnp.int32)
    order = (iota((rows, rows), 0) == target).astype(F32).astype(BF16)

    shells = shell_ref[...].reshape(rows, halves * LANES).astype(F32).astype(BF16)
    moved = jnp.dot(order, shells, preferred_element_type=F32)
    meta = sum(jnp.dot(order, part, preferred_element_type=F32) for part in three_parts(columns))
    for group in range(devices // 8):
        base = group * 8 * stride
        total = jnp.zeros((8, LANES), F32)
        for c in range(per_peer):
            first = c * devices + group * 8
            for h in range(halves):
                out_ref[pl.ds(base + c * halves + h, 8, stride=stride), :] = moved[
                    first : first + 8, h * LANES : (h + 1) * LANES
                ]
            piece = meta[first : first + 8, :]
            total = total + (pltpu.roll(piece, FIELDS * c, 1) if c else piece)
        out_ref[pl.ds(base + stride - 1, 8, stride=stride), :] = total

    odd = lax.bitwise_and(iota((8, LANES), 0), 1) == 1
    slot_rank = iota((slots, 1), 0)
    for b in range(batches):
        squared = jnp.zeros((slots, halves * LANES), F32)
        for axis in range(3):
            place = columns[b * slots : (b + 1) * slots, axis : axis + 1]
            offset = coord_ref[axis, b : b + 1, :] - place
            squared = squared + offset * offset
        close = jnp.where(slot_rank < count_ref[b], 1.0 / (1.0 + squared), 0.0)
        live = jnp.where(load_ref[0] > b, 1.0, 0.0)
        weight = charge_ref[b : b + 1, :] * live / jnp.sum(close, axis=0, keepdims=True)
        for quantity in range(4):
            line = coord_ref[quantity, b : b + 1, :] if quantity < 3 else weight
            value = jnp.where(odd, line[:, LANES : 2 * LANES], line[:, 0:LANES])
            for group in range(devices // 8):
                at = group * 8 * stride + per_peer * halves + b * 4 + quantity
                out_ref[pl.ds(at, 8, stride=stride), :] = value


def harmonics(x, y, z):
    def factor(degree, azimuth):
        norm = math.sqrt(
            (2 * degree + 1) / (4 * math.pi) * math.factorial(degree - azimuth) / math.factorial(degree + azimuth)
        )
        return norm * (math.sqrt(2.0) if azimuth else 1.0)

    cosine, sine = None, None
    for azimuth in range(LMAX + 1):
        if azimuth == 1:
            cosine, sine = x, y
        elif azimuth > 1:
            cosine, sine = cosine * x - sine * y, cosine * y + sine * x
        older, newer = None, None
        for degree in range(azimuth, LMAX + 1):
            if degree == azimuth:
                value = float(math.prod(range(1, 2 * azimuth, 2))) * factor(degree, azimuth)
            elif degree == azimuth + 1:
                value = z * ((2 * azimuth + 1) * newer / factor(degree - 1, azimuth) * factor(degree, azimuth))
            else:
                up = (2 * degree - 1) / (degree - azimuth) * factor(degree, azimuth) / factor(degree - 1, azimuth)
                down = (degree + azimuth - 1) / (degree - azimuth) * factor(degree, azimuth) / factor(degree - 2, azimuth)
                value = (z * up) * newer - down * older
            older, newer = newer, value
            middle = degree * degree + degree
            if azimuth == 0:
                yield middle, value
            else:
                yield middle + azimuth, cosine * value
                yield middle - azimuth, sine * value


def two_parts(value):
    first = value.astype(BF16).astype(F32)
    return first, value - first


def owner_kernel(
    devices,
    per_peer,
    batches,
    parity_ref,
    own_ref,
    other_ref,
    moment_ref,
    reply_ref,
    y_own,
    y_other,
    w_own,
    w_other,
    hot_ref,
    sum_ref,
    table_ref,
    split_ref,
    part_own,
    part_other,
    meta_ref,
    meta_smem,
    sem,
):
    stride = own_ref.shape[0] // devices
    groups = devices // 8
    rows = devices * per_peer
    owned = moment_ref.shape[0]
    shell_rows = per_peer * 2
    parity = parity_ref[0]

    def gather_meta(group, carry):
        at = pl.multiple_of(group * 8, 8)
        line = own_ref[pl.ds(group * 8 * stride + stride - 1, 8, stride=stride), :]
        meta_ref[pl.ds(at, 8), :] = line.astype(jnp.int32)
        return carry

    lax.fori_loop(0, groups, gather_meta, 0)
    copy = pltpu.make_async_copy(meta_ref, meta_smem, sem)
    copy.start()

    sum_ref[...] = jnp.zeros_like(sum_ref)
    table_ref[...] = jnp.zeros_like(table_ref)

    def column(line, c, field):
        at = FIELDS * c + field
        return jnp.broadcast_to(line[:, at : at + 1], (8, LANES))

    def geometry(group, carry):
        base = group * 8 * stride
        line = own_ref[pl.ds(base + stride - 1, 8, stride=stride), :]
        for source, y_ref, w_ref in ((own_ref, y_own, w_own), (other_ref, y_other, w_other)):
            points = [
                [source[pl.ds(base + shell_rows + b * 4 + i, 8, stride=stride), :] for i in range(4)]
                for b in range(batches)
            ]
            for c in range(per_peer):
                batch = column(line, c, 4)
                chosen = list(points[0])
                for b in range(1, batches):
                    chosen = [jnp.where(batch == b, new, old) for new, old in zip(points[b], chosen)]
                offset = [chosen[i] - column(line, c, i) for i in range(3)]
                squared = offset[0] * offset[0] + offset[1] * offset[1] + offset[2] * offset[2]
                scale = lax.rsqrt(squared + SOFTEN)
                weight = jnp.where(column(line, c, 5) > 0.5, chosen[3] / (1.0 + squared), 0.0)
                w_ref[pl.ds(group * 8 * per_peer + c, 8, stride=per_peer), :] = weight
                start = (group * 8 * per_peer + c) * PAD
                for k, value in harmonics(*(part * scale for part in offset)):
                    y_ref[pl.ds(start + k, 8, stride=per_peer * PAD), :] = jnp.broadcast_to(value, (8, LANES))
                for k in range(HARM, PAD):
                    y_ref[pl.ds(start + k, 8, stride=per_peer * PAD), :] = jnp.zeros((8, LANES), F32)
        return carry

    lax.fori_loop(0, groups, geometry, 0)
    copy.wait()

    def forward(source, carry):
        for c in range(per_peer):
            row = source * per_peer + c
            first = pl.multiple_of(row * PAD, 8)
            weighted, hot = [], []
            for side, (y_ref, w_ref) in enumerate(((y_own, w_own), (y_other, w_other))):
                weighted.append(y_ref[pl.ds(first, PAD), :] * w_ref[pl.ds(row, 1), :])
                half = parity if side == 0 else 1 - parity
                shell = own_ref[pl.ds(source * stride + c * 2 + half, 1), :]
                hot.append((iota((SHELLS, LANES), 0).astype(F32) == shell).astype(F32))
            weighted = jnp.concatenate(weighted, axis=1).reshape(PAD // 8, 8, 2 * LANES)
            hot = jnp.concatenate(hot, axis=1).astype(BF16)
            hot_ref[pl.ds(pl.multiple_of(row * SHELLS, SHELLS), SHELLS), :] = hot
            both = jnp.concatenate(two_parts(weighted), axis=1).reshape(2 * PAD, 2 * LANES).astype(BF16)
            made = lax.dot_general(both, hot, (((1,), (1,)), ((), ())), preferred_element_type=F32)
            made = made.reshape(PAD // 8, 2, 8, SHELLS)
            made = (made[:, 0] + made[:, 1]).reshape(PAD, SHELLS)
            local = meta_smem[source, FIELDS * c + 3]
            at = pl.multiple_of(local * PAD, 8)
            sum_ref[pl.ds(at, PAD), 0:SHELLS] += made
        return carry

    lax.fori_loop(0, devices, forward, 0)

    left = iota((owned, LANES), 1) < SHELLS
    row_rank = iota((SHELLS, LANES), 0).astype(F32)
    lane_rank = iota((SHELLS, LANES), 1).astype(F32)
    ratio = jnp.exp(jnp.abs(row_rank - lane_rank) * (-2.3 / SHELLS))
    kernel = jnp.exp(jnp.maximum(row_rank, lane_rank) * (-2.3 / SHELLS)) * 2.0
    kernel = jnp.where(lane_rank < SHELLS, kernel, 0.0)
    before = None
    for degree in range(LMAX + 1):
        lines = []
        for k in range(degree * degree, (degree + 1) ** 2):
            line = sum_ref[pl.ds(k, owned, stride=PAD), :]
            lines.append(line)
            if k % 2 == 0:
                before = line
                if k == HARM - 1:
                    moment_ref[:, k * SHELLS : (k + 1) * SHELLS] = line[:, 0:SHELLS]
            else:
                moment_ref[:, (k - 1) * SHELLS : (k + 1) * SHELLS] = jnp.where(
                    left, before, pltpu.roll(line, SHELLS, 1)
                )
        green = kernel * (4.0 * math.pi / (2 * degree + 1))
        kernel = kernel * ratio
        g_first, g_second = two_parts(green)
        first, second = two_parts(jnp.concatenate(lines, axis=0))
        both = (first + pltpu.roll(second, SHELLS, 1)).astype(BF16)
        made = jnp.dot(both, jnp.concatenate([g_first, g_first], axis=0).astype(BF16), preferred_element_type=F32)
        made = made + jnp.dot(
            both, jnp.concatenate([g_second, g_second], axis=0).astype(BF16), preferred_element_type=F32
        )
        for place, k in enumerate(range(degree * degree, (degree + 1) ** 2)):
            table_ref[pl.ds(k, owned, stride=PAD), :] = made[place * owned : (place + 1) * owned, :]

    def split(atom, carry):
        first, second = two_parts(table_ref[pl.ds(pl.multiple_of(atom * PAD, 8), PAD), :])
        both = first + pltpu.roll(second, SHELLS, 1)
        both = jnp.concatenate([both, jnp.zeros((SHELLS - PAD, LANES), F32)], axis=0)
        split_ref[pl.ds(pl.multiple_of(atom * SHELLS, SHELLS), SHELLS), :] = both.astype(BF16)
        return carry

    lax.fori_loop(0, owned, split, 0)

    def evaluate(source, carry):
        for c in range(per_peer):
            row = source * per_peer + c
            local = meta_smem[source, FIELDS * c + 3]
            table = split_ref[pl.ds(pl.multiple_of(local * SHELLS, SHELLS), SHELLS), :]
            hot = hot_ref[pl.ds(pl.multiple_of(row * SHELLS, SHELLS), SHELLS), :]
            picked = jnp.dot(table, jnp.concatenate([hot, hot], axis=0), preferred_element_type=F32)
            first = pl.multiple_of(row * PAD, 8)
            at = pl.multiple_of(row * 8, 8)
            for side, (y_ref, part_ref) in enumerate(((y_own, part_own), (y_other, part_other))):
                product = picked[0:PAD, side * LANES : (side + 1) * LANES] * y_ref[pl.ds(first, PAD), :]
                part_ref[pl.ds(at, 8), :] = jnp.sum(product.reshape(PAD // 8, 8, LANES), axis=0)
        return carry

    lax.fori_loop(0, devices, evaluate, 0)

    def answer(group, carry):
        line = own_ref[pl.ds(group * 8 * stride + stride - 1, 8, stride=stride), :]
        for side, part_ref in enumerate((part_own, part_other)):
            half = parity if side == 0 else 1 - parity
            totals = [jnp.zeros((8, LANES), F32) for _ in range(batches)]
            for c in range(per_peer):
                start = (group * 8 * per_peer + c) * 8
                total = part_ref[pl.ds(start, 8, stride=per_peer * 8), :]
                for i in range(1, 8):
                    total = total + part_ref[pl.ds(start + i, 8, stride=per_peer * 8), :]
                total = jnp.where(column(line, c, 5) > 0.5, total, 0.0)
                batch = column(line, c, 4)
                totals = [old + jnp.where(batch == b, total, 0.0) for b, old in enumerate(totals)]
            for b in range(batches):
                at = group * 8 * (2 * batches) + half * batches + b
                reply_ref[pl.ds(at, 8, stride=2 * batches), :] = totals[b]
        return carry

    lax.fori_loop(0, groups, answer, 0)


def body(
    point_coords,
    charge,
    shell_index,
    neighbours,
    neighbour_count,
    batch_load,
    atom_coords,
    owner_slot,
):
    batches, slots = neighbours.shape
    points = charge.shape[1]
    atoms = owner_slot.shape[0]
    count_gy = lax.axis_size("gy")
    devices = lax.axis_size("gx") * count_gy
    owned = atoms // devices
    rows = batches * slots
    per_peer = rows // devices
    stride = per_peer * (points // LANES) + batches * 4 + 1

    outgoing = pl.pallas_call(
        functools.partial(pack_kernel, devices),
        out_shape=jax.ShapeDtypeStruct((devices * stride, LANES), F32),
        in_specs=[SMEM, SMEM] + [VMEM] * 6,
        out_specs=VMEM,
        scratch_shapes=[pltpu.VMEM((8, atoms), F32)],
        name="pack",
    )(
        neighbour_count,
        batch_load,
        neighbours,
        jnp.transpose(point_coords, (1, 0, 2)),
        charge,
        shell_index,
        atom_coords,
        owner_slot.reshape(atoms // LANES, LANES),
    )
    arrived = lax.all_to_all(
        outgoing.reshape(devices, stride, 1, LANES), ("gx", "gy"), split_axis=0, concat_axis=0, tiled=True
    ).reshape(devices * stride, LANES)
    swapped = lax.ppermute(arrived, "gy", [(i, i ^ 1) for i in range(count_gy)])
    parity = (lax.axis_index("gy") % 2).astype(jnp.int32).reshape(1)
    moments, reply = pl.pallas_call(
        functools.partial(owner_kernel, devices, per_peer, batches),
        out_shape=(
            jax.ShapeDtypeStruct((owned, HARM * SHELLS), F32),
            jax.ShapeDtypeStruct((devices * 2 * batches, LANES), F32),
        ),
        in_specs=[SMEM, VMEM, VMEM],
        out_specs=(VMEM, VMEM),
        scratch_shapes=[
            pltpu.VMEM((rows * PAD, LANES), F32),
            pltpu.VMEM((rows * PAD, LANES), F32),
            pltpu.VMEM((rows, LANES), F32),
            pltpu.VMEM((rows, LANES), F32),
            pltpu.VMEM((rows * SHELLS, 2 * LANES), BF16),
            pltpu.VMEM((owned * PAD, LANES), F32),
            pltpu.VMEM((owned * PAD, LANES), F32),
            pltpu.VMEM((owned * SHELLS, LANES), BF16),
            pltpu.VMEM((rows * 8, LANES), F32),
            pltpu.VMEM((rows * 8, LANES), F32),
            pltpu.VMEM((devices, LANES), jnp.int32),
            pltpu.SMEM((devices, LANES), jnp.int32),
            pltpu.SemaphoreType.DMA,
        ],
        compiler_params=pltpu.CompilerParams(vmem_limit_bytes=24 << 20),
        name="owner",
    )(parity, arrived, swapped)
    returned = lax.all_to_all(
        reply.reshape(devices, 2 * batches, LANES), ("gx", "gy"), split_axis=0, concat_axis=0, tiled=True
    )
    potential = jnp.sum(returned, axis=0).reshape(2, batches, LANES)
    return jnp.transpose(potential, (1, 0, 2)).reshape(batches, points), moments


def solution(mesh):
    return jax.shard_map(
        body,
        mesh=mesh,
        in_specs=(
            P(("gx", "gy"), None, None),
            P(("gx", "gy"), None),
            P(("gx", "gy"), None, None),
            P(("gx", "gy"), None),
            P(("gx", "gy")),
            P(("gx", "gy")),
            P(),
            P(),
        ),
        out_specs=(P(("gx", "gy"), None), P(("gx", "gy"), None)),
        check_vma=False,
    )
```

time: 208 us -> 59.5 us (0.29)
  waiting for transfers between devices: 77.4 us -> 1.63 us
  local copies, waits for them, and re-layouts: 55.9 us -> 0 us
  blocking collectives: 0 us -> 31.4 us
  matrix products: 29.5 us -> 0 us
  Pallas kernels: 0 us -> 24.2 us
  other arithmetic: 24.1 us -> 0.63 us
  starting transfers between devices: 16 us -> 0.12 us
    all_to_all x3 -> x0, waiting for transfers between devices: 77.4 us -> none  [the longest x1 40.1 us: body(): lax.all_to_all(reply, ('gx', 'gy'), split_axis=0, concat_axis=0, tiled=True)]
    all_to_all x0 -> x2, blocking collectives: none -> 31.4 us  [the longest x1 21.1 us: body(): lax.all_to_all(outgoing.reshape(devices, stride, 1, LANES), ('gx', 'gy'),...]
    dot_general x10 -> x0, matrix products: 29.5 us -> none  [the longest x4 13 us: evaluate(): picked = jnp.einsum('jls,jps->jlp', table_rows, selector, precision=HIGHEST)]
    pallas_call x0 -> x2, Pallas kernels: none -> 24.2 us  [the longest x1 21.8 us: body(): pl.pallas_call(functools.partial(owner_kernel, devices, per_peer, batches...]
    dynamic_slice x32 -> x0, local copies, waits for them, and re-layouts: 21.5 us -> none  [the longest x28 15.4 us: body(): lax.map(forward, (point_coords, charge, shell_index, neighbours, neighbou...]
    all_to_all x3 -> x0, starting transfers between devices: 16 us -> none  [the longest x1 7.33 us: body(): lax.all_to_all(labels_out, ('gx', 'gy'), split_axis=0, concat_axis=0, til...]
    dynamic_update_slice x8 -> x0, local copies, waits for them, and re-layouts: 10.3 us -> none  [the longest x4 5.22 us: body(): lax.map(evaluate, (fetched, harmonic, shell_index, neighbour_count, live_...]
    reshape x5 -> x0, local copies, waits for them, and re-layouts: 7.29 us -> none  [the longest x1 3.91 us: body(): rows_flat = partial_value.reshape(batches * slots, width)]
  transfers between devices with their start and end apart: 3 -> 1, of which waited for: 2 -> 1; matrix products, arithmetic and copies ran while one was open for 27% -> 0% of each run, Pallas kernels for 0% -> 0%
where the time goes in v1:
time: 59.5 us; the launch traced here: 59.2 us
  blocking collectives  31.4 us (53%)
  Pallas kernels  24.2 us (41%)
  waiting for transfers between devices  1.63 us (3%)
  between operations  1.29 us (2%)
  other arithmetic  0.63 us (1%)
    pallas_call x1, Pallas kernels, body(): pl.pallas_call(functools.partial(owner_kernel, devices, per_peer, batches...  21.8 us
    all_to_all x1, blocking collectives, body(): lax.all_to_all(outgoing.reshape(devices, stride, 1, LANES), ('gx', 'gy'),...  21.1 us
    all_to_all x1, blocking collectives, body(): lax.all_to_all(reply.reshape(devices, 2 * batches, LANES), ('gx', 'gy'),...  10.3 us
    pallas_call x1, Pallas kernels, body(): pl.pallas_call(functools.partial(pack_kernel, devices), out_shape=jax.Sha...  2.32 us
    ppermute x1, waiting for transfers between devices, body(): swapped = lax.ppermute(arrived, 'gy', [(i, i ^ 1) for i in range(count_gy)])  1.63 us
  transfers between devices with their start and end apart: 1, of which 1 were waited for; matrix products, arithmetic and copies ran while one was open for 0% of the time, Pallas kernels for 0%

profile of v1, /device:TPU:0, one launch (start us, length us, event | category | flops | bytes accessed | tf_op | source)
XLA Modules:
  0.0 59.2 jit_solution(6809931601044142484)
XLA Ops:
  1.3 2.3 %pack.1 = f32[800,128]{1,0:T(8,128)} custom-call(s32[4]{0:T(128)} %count_ref.1, s32[1]{0:T(128)S(6)} %copy.11.load_ref, s32[4,32]{1,0:T(4,128)} %label_ref.1, f32[3,4,256]{2,1,0:T(4,128)} %bitcast.15, f32[4,256]{1,0:T(4,128)} %charge_ref.1, s32[4,32,256]{2,1,0:T(8,128)} %shell_ref.1, f32[3,1024]{1,0:T(4,128)} %atom_ref.1, s32[8,128]{1,0:T(8,128)} %bitcast.16), custom_call_target="tpu_custom_call" | custom-call | tf_op jit(solution)/shard_map/pack/pallas_call | solution.py:353
  3.6 21.1 %all_to_all.10 = f32[32,25,1,128]{3,2,1,0:T(1,128)S(1)} all-to-all(f32[32,25,1,128]{3,2,1,0:T(1,128)} %bitcast.14), channel_id=1, replica_groups=mesh['gx'=4,'gy'=8] {'gx','gy'}, dimensions={0} | all-to-all | bytes 819200 | tf_op jit(solution)/shard_map/all_to_all | solution.py:370
  24.7 0.1 collective-permute-start
  24.8 1.6 %collective-permute-done.other_ref = f32[800,128]{1,0:T(8,128)S(1)} collective-permute-done((f32[800,128]{1,0:T(8,128)S(1)}, f32[800,128]{1,0:T(8,128)S(1)}, u32[]{:S(2)}, u32[]{:S(2)}) %collective-permute-start) | collective-permute-done | bytes 409632 | tf_op jit(solution)/shard_map/ppermute | solution.py:373
  26.5 21.8 %owner.1 = (f32[32,3136]{1,0:T(8,128)}, f32[256,128]{1,0:T(8,128)S(1)}) custom-call(s32[1]{0:T(128)} %bitcast.parity_ref, f32[800,128]{1,0:T(8,128)S(1)} %bitcast.12, f32[800,128]{1,0:T(8,128)S(1)} %collective-permute-done.other_ref), custom_call_target="tpu_custom_call" | custom-call | tf_op jit(solution)/shard_map/owner/pallas_call | solution.py:375
  48.3 10.3 %all_to_all.11 = f32[32,8,128]{2,1,0:T(8,128)S(1)} all-to-all(f32[32,8,128]{2,1,0:T(8,128)S(1)} %bitcast.13), channel_id=1, replica_groups=mesh['gx'=4,'gy'=8] {'gx','gy'}, dimensions={0} | all-to-all | bytes 262144 | tf_op jit(solution)/shard_map/all_to_all | solution.py:401
  58.6 0.6 %reduce_sum.9 = f32[8,128]{1,0:T(8,128)} reduce(f32[32,8,128]{2,1,0:T(8,128)S(1)} %all_to_all.11, f32[]{:T(128)} %constant.18.clone.1), dimensions={0}, to_apply=%region_0.1 | reduce | flops 31744 | bytes 135172 | tf_op jit(solution)/shard_map/reduce_sum | solution.py:404
Async XLA Ops:
  24.7 1.7 %collective-permute-start = (f32[800,128]{1,0:T(8,128)S(1)}, f32[800,128]{1,0:T(8,128)S(1)}, u32[]{:S(2)}, u32[]{:S(2)}) collective-permute-start(f32[800,128]{1,0:T(8,128)S(1)} %bitcast.11), channel_id=1, source_target_pairs={{0,1},{1,0},{2,3},{3,2},{4,5},{5,4},{6,7},{7,6},{8,9},{9,8},{10,11... | collective-permute-start | bytes 1228808 | tf_op jit(solution)/shard_map/ppermute | solution.py:373

commit v2 on v1

--- a/solution.py
+++ b/solution.py
@@ -15,6 +15,9 @@
 SOFTEN = 0.01
 LANES = 128
 FIELDS = 8
+BLOCK = 448
+SPILL = 64
+ROWS_AT_ONCE = 16
 VMEM = pl.BlockSpec(memory_space=pltpu.VMEM)
 SMEM = pl.BlockSpec(memory_space=pltpu.SMEM)
 F32 = jnp.float32
@@ -148,6 +151,20 @@
                 yield middle - azimuth, sine * value
 
 
+def split_rows(value):
+    main, tail = value[0 : PAD - 8], value[PAD - 8 : PAD]
+    first = main.astype(BF16)
+    second = (main - first.astype(F32)).astype(BF16)
+    last = tail.astype(BF16).astype(F32)
+    last = jnp.concatenate([last, tail - last], axis=0).astype(BF16)
+    return jnp.concatenate([first, last, second], axis=0)
+
+
+def join_rows(value):
+    main = value[0 : PAD - 8] + value[PAD + 8 :]
+    return jnp.concatenate([main, value[PAD - 8 : PAD] + value[PAD : PAD + 8]], axis=0)
+
+
 def two_parts(value):
     first = value.astype(BF16).astype(F32)
     return first, value - first
@@ -160,28 +177,30 @@
     parity_ref,
     own_ref,
     other_ref,
-    moment_ref,
+    moment_hbm,
     reply_ref,
     y_own,
     y_other,
     w_own,
     w_other,
-    hot_ref,
     sum_ref,
     table_ref,
     split_ref,
     part_own,
     part_other,
+    moment_ref,
     meta_ref,
     meta_smem,
     sem,
+    out_sem,
 ):
     stride = own_ref.shape[0] // devices
     groups = devices // 8
-    rows = devices * per_peer
     owned = moment_ref.shape[0]
+    pitch = owned + 1
     shell_rows = per_peer * 2
     parity = parity_ref[0]
+    step = max(1, ROWS_AT_ONCE // per_peer)
 
     def gather_meta(group, carry):
         at = pl.multiple_of(group * 8, 8)
@@ -195,6 +214,8 @@
 
     sum_ref[...] = jnp.zeros_like(sum_ref)
     table_ref[...] = jnp.zeros_like(table_ref)
+    for y_ref in (y_own, y_other):
+        y_ref[pl.ds(devices * per_peer // 8 * BLOCK, SPILL), :] = jnp.zeros((SPILL, LANES), F32)
 
     def column(line, c, field):
         at = FIELDS * c + field
@@ -218,39 +239,43 @@
                 scale = lax.rsqrt(squared + SOFTEN)
                 weight = jnp.where(column(line, c, 5) > 0.5, chosen[3] / (1.0 + squared), 0.0)
                 w_ref[pl.ds(group * 8 * per_peer + c, 8, stride=per_peer), :] = weight
-                start = (group * 8 * per_peer + c) * PAD
+                start = pl.multiple_of((group * per_peer + c) * BLOCK, 8)
                 for k, value in harmonics(*(part * scale for part in offset)):
-                    y_ref[pl.ds(start + k, 8, stride=per_peer * PAD), :] = jnp.broadcast_to(value, (8, LANES))
-                for k in range(HARM, PAD):
-                    y_ref[pl.ds(start + k, 8, stride=per_peer * PAD), :] = jnp.zeros((8, LANES), F32)
+                    y_ref[pl.ds(start + k * 9, 8), :] = jnp.broadcast_to(value, (8, LANES))
         return carry
 
     lax.fori_loop(0, groups, geometry, 0)
     copy.wait()
 
-    def forward(source, carry):
-        for c in range(per_peer):
+    def hot_shells(source, c):
+        hot = []
+        for side in range(2):
+            half = parity if side == 0 else 1 - parity
+            shell = own_ref[pl.ds(source * stride + c * 2 + half, 1), :]
+            hot.append((iota((SHELLS, LANES), 0).astype(F32) == shell).astype(F32))
+        return jnp.concatenate(hot, axis=1).astype(BF16)
+
+    def harmonic_rows(source, c, y_ref):
+        start = ((source // 8) * per_peer + c) * BLOCK + source % 8
+        return y_ref[pl.ds(start, PAD, stride=9), :]
+
+    def forward(turn, carry):
+        for place in range(step * per_peer):
+            source, c = turn * step + place // per_peer, place % per_peer
             row = source * per_peer + c
-            first = pl.multiple_of(row * PAD, 8)
-            weighted, hot = [], []
-            for side, (y_ref, w_ref) in enumerate(((y_own, w_own), (y_other, w_other))):
-                weighted.append(y_ref[pl.ds(first, PAD), :] * w_ref[pl.ds(row, 1), :])
-                half = parity if side == 0 else 1 - parity
-                shell = own_ref[pl.ds(source * stride + c * 2 + half, 1), :]
-                hot.append((iota((SHELLS, LANES), 0).astype(F32) == shell).astype(F32))
-            weighted = jnp.concatenate(weighted, axis=1).reshape(PAD // 8, 8, 2 * LANES)
-            hot = jnp.concatenate(hot, axis=1).astype(BF16)
-            hot_ref[pl.ds(pl.multiple_of(row * SHELLS, SHELLS), SHELLS), :] = hot
-            both = jnp.concatenate(two_parts(weighted), axis=1).reshape(2 * PAD, 2 * LANES).astype(BF16)
-            made = lax.dot_general(both, hot, (((1,), (1,)), ((), ())), preferred_element_type=F32)
-            made = made.reshape(PAD // 8, 2, 8, SHELLS)
-            made = (made[:, 0] + made[:, 1]).reshape(PAD, SHELLS)
+            weighted = [
+                harmonic_rows(source, c, y_ref) * w_ref[pl.ds(row, 1), :]
+                for y_ref, w_ref in ((y_own, w_own), (y_other, w_other))
+            ]
+            both = split_rows(jnp.concatenate(weighted, axis=1))
+            made = lax.dot_general(
+                both, hot_shells(source, c), (((1,), (1,)), ((), ())), preferred_element_type=F32
+            )
             local = meta_smem[source, FIELDS * c + 3]
-            at = pl.multiple_of(local * PAD, 8)
-            sum_ref[pl.ds(at, PAD), 0:SHELLS] += made
-        return carry
-
-    lax.fori_loop(0, devices, forward, 0)
+            sum_ref[pl.ds(local, PAD, stride=pitch), 0:SHELLS] += join_rows(made)
+        return carry
+
+    lax.fori_loop(0, devices // step, forward, 0)
 
     left = iota((owned, LANES), 1) < SHELLS
     row_rank = iota((SHELLS, LANES), 0).astype(F32)
@@ -262,7 +287,7 @@
     for degree in range(LMAX + 1):
         lines = []
         for k in range(degree * degree, (degree + 1) ** 2):
-            line = sum_ref[pl.ds(k, owned, stride=PAD), :]
+            line = sum_ref[k * pitch : k * pitch + owned, :]
             lines.append(line)
             if k % 2 == 0:
                 before = line
@@ -282,32 +307,32 @@
             both, jnp.concatenate([g_second, g_second], axis=0).astype(BF16), preferred_element_type=F32
         )
         for place, k in enumerate(range(degree * degree, (degree + 1) ** 2)):
-            table_ref[pl.ds(k, owned, stride=PAD), :] = made[place * owned : (place + 1) * owned, :]
-
-    def split(atom, carry):
-        first, second = two_parts(table_ref[pl.ds(pl.multiple_of(atom * PAD, 8), PAD), :])
-        both = first + pltpu.roll(second, SHELLS, 1)
-        both = jnp.concatenate([both, jnp.zeros((SHELLS - PAD, LANES), F32)], axis=0)
-        split_ref[pl.ds(pl.multiple_of(atom * SHELLS, SHELLS), SHELLS), :] = both.astype(BF16)
-        return carry
-
-    lax.fori_loop(0, owned, split, 0)
-
-    def evaluate(source, carry):
-        for c in range(per_peer):
-            row = source * per_peer + c
+            table_ref[k * pitch : k * pitch + owned, :] = made[place * owned : (place + 1) * owned, :]
+    result = pltpu.make_async_copy(moment_ref, moment_hbm, out_sem)
+    result.start()
+
+    def split(turn, carry):
+        for place in range(8):
+            atom = turn * 8 + place
+            both = split_rows(table_ref[pl.ds(atom, PAD, stride=pitch), :])
+            split_ref[pl.ds(pl.multiple_of(atom * 2 * PAD, 16), 2 * PAD), :] = both
+        return carry
+
+    lax.fori_loop(0, owned // 8, split, 0)
+
+    def evaluate(turn, carry):
+        for place in range(step * per_peer):
+            source, c = turn * step + place // per_peer, place % per_peer
             local = meta_smem[source, FIELDS * c + 3]
-            table = split_ref[pl.ds(pl.multiple_of(local * SHELLS, SHELLS), SHELLS), :]
-            hot = hot_ref[pl.ds(pl.multiple_of(row * SHELLS, SHELLS), SHELLS), :]
-            picked = jnp.dot(table, jnp.concatenate([hot, hot], axis=0), preferred_element_type=F32)
-            first = pl.multiple_of(row * PAD, 8)
-            at = pl.multiple_of(row * 8, 8)
+            table = split_ref[pl.ds(pl.multiple_of(local * 2 * PAD, 16), 2 * PAD), 0:SHELLS]
+            picked = join_rows(jnp.dot(table, hot_shells(source, c), preferred_element_type=F32))
+            at = ((source // 8) * per_peer + c) * 72 + source % 8
             for side, (y_ref, part_ref) in enumerate(((y_own, part_own), (y_other, part_other))):
-                product = picked[0:PAD, side * LANES : (side + 1) * LANES] * y_ref[pl.ds(first, PAD), :]
-                part_ref[pl.ds(at, 8), :] = jnp.sum(product.reshape(PAD // 8, 8, LANES), axis=0)
-        return carry
-
-    lax.fori_loop(0, devices, evaluate, 0)
+                product = picked[:, side * LANES : (side + 1) * LANES] * harmonic_rows(source, c, y_ref)
+                part_ref[pl.ds(at, 8, stride=9), :] = jnp.sum(product.reshape(PAD // 8, 8, LANES), axis=0)
+        return carry
+
+    lax.fori_loop(0, devices // step, evaluate, 0)
 
     def answer(group, carry):
         line = own_ref[pl.ds(group * 8 * stride + stride - 1, 8, stride=stride), :]
@@ -315,10 +340,10 @@
             half = parity if side == 0 else 1 - parity
             totals = [jnp.zeros((8, LANES), F32) for _ in range(batches)]
             for c in range(per_peer):
-                start = (group * 8 * per_peer + c) * 8
-                total = part_ref[pl.ds(start, 8, stride=per_peer * 8), :]
+                start = pl.multiple_of((group * per_peer + c) * 72, 8)
+                total = part_ref[pl.ds(start, 8), :]
                 for i in range(1, 8):
-                    total = total + part_ref[pl.ds(start + i, 8, stride=per_peer * 8), :]
+                    total = total + part_ref[pl.ds(start + 9 * i, 8), :]
                 total = jnp.where(column(line, c, 5) > 0.5, total, 0.0)
                 batch = column(line, c, 4)
                 totals = [old + jnp.where(batch == b, total, 0.0) for b, old in enumerate(totals)]
@@ -328,6 +353,7 @@
         return carry
 
     lax.fori_loop(0, groups, answer, 0)
+    result.wait()
 
 
 def body(
@@ -379,20 +405,21 @@
             jax.ShapeDtypeStruct((devices * 2 * batches, LANES), F32),
         ),
         in_specs=[SMEM, VMEM, VMEM],
-        out_specs=(VMEM, VMEM),
+        out_specs=(pl.BlockSpec(memory_space=pltpu.HBM), VMEM),
         scratch_shapes=[
-            pltpu.VMEM((rows * PAD, LANES), F32),
-            pltpu.VMEM((rows * PAD, LANES), F32),
+            pltpu.VMEM((rows // 8 * BLOCK + SPILL, LANES), F32),
+            pltpu.VMEM((rows // 8 * BLOCK + SPILL, LANES), F32),
             pltpu.VMEM((rows, LANES), F32),
             pltpu.VMEM((rows, LANES), F32),
-            pltpu.VMEM((rows * SHELLS, 2 * LANES), BF16),
-            pltpu.VMEM((owned * PAD, LANES), F32),
-            pltpu.VMEM((owned * PAD, LANES), F32),
-            pltpu.VMEM((owned * SHELLS, LANES), BF16),
-            pltpu.VMEM((rows * 8, LANES), F32),
-            pltpu.VMEM((rows * 8, LANES), F32),
+            pltpu.VMEM((PAD * (owned + 1), LANES), F32),
+            pltpu.VMEM((PAD * (owned + 1), LANES), F32),
+            pltpu.VMEM((owned * 2 * PAD, LANES), BF16),
+            pltpu.VMEM((rows * 9, LANES), F32),
+            pltpu.VMEM((rows * 9, LANES), F32),
+            pltpu.VMEM((owned, HARM * SHELLS), F32),
             pltpu.VMEM((devices, LANES), jnp.int32),
             pltpu.SMEM((devices, LANES), jnp.int32),
+            pltpu.SemaphoreType.DMA,
             pltpu.SemaphoreType.DMA,
         ],
         compiler_params=pltpu.CompilerParams(vmem_limit_bytes=24 << 20),

time: 59.5 us -> 46.1 us (0.77)
  Pallas kernels: 24.2 us -> 10.8 us
    pallas_call x1, Pallas kernels: 21.8 us -> 8.5 us  [body(): pl.pallas_call(functools.partial(owner_kernel, devices, per_peer, batches...]
where the time goes in v2:
time: 46.1 us; the launch traced here: 45.8 us
  blocking collectives  31.4 us (68%)
  Pallas kernels  10.8 us (23%)
  waiting for transfers between devices  1.63 us (4%)
  between operations  1.29 us (3%)
  other arithmetic  0.63 us (1%)
    all_to_all x1, blocking collectives, body(): lax.all_to_all(outgoing.reshape(devices, stride, 1, LANES), ('gx', 'gy'),...  21.1 us
    all_to_all x1, blocking collectives, body(): lax.all_to_all(reply.reshape(devices, 2 * batches, LANES), ('gx', 'gy'),...  10.3 us
    pallas_call x1, Pallas kernels, body(): pl.pallas_call(functools.partial(owner_kernel, devices, per_peer, batches...  8.5 us
    pallas_call x1, Pallas kernels, body(): pl.pallas_call(functools.partial(pack_kernel, devices), out_shape=jax.Sha...  2.32 us
    ppermute x1, waiting for transfers between devices, body(): swapped = lax.ppermute(arrived, 'gy', [(i, i ^ 1) for i in range(count_gy)])  1.63 us
  transfers between devices with their start and end apart: 1, of which 1 were waited for; matrix products, arithmetic and copies ran while one was open for 0% of the time, Pallas kernels for 0%

profile of v2, /device:TPU:0, one launch (start us, length us, event | category | flops | bytes accessed | tf_op | source)
XLA Modules:
  0.0 45.8 jit_solution(681833763398464246)
XLA Ops:
  1.3 2.3 %pack.1 = f32[800,128]{1,0:T(8,128)} custom-call(s32[4]{0:T(128)} %count_ref.1, s32[1]{0:T(128)S(6)} %copy.11.load_ref, s32[4,32]{1,0:T(4,128)} %label_ref.1, f32[3,4,256]{2,1,0:T(4,128)} %bitcast.15, f32[4,256]{1,0:T(4,128)} %charge_ref.1, s32[4,32,256]{2,1,0:T(8,128)} %shell_ref.1, f32[3,1024]{1,0:T(4,128)} %atom_ref.1, s32[8,128]{1,0:T(8,128)} %bitcast.16), custom_call_target="tpu_custom_call" | custom-call | tf_op jit(solution)/shard_map/pack/pallas_call | solution.py:379
  3.6 21.1 %all_to_all.10 = f32[32,25,1,128]{3,2,1,0:T(1,128)S(1)} all-to-all(f32[32,25,1,128]{3,2,1,0:T(1,128)} %bitcast.14), channel_id=1, replica_groups=mesh['gx'=4,'gy'=8] {'gx','gy'}, dimensions={0} | all-to-all | bytes 819200 | tf_op jit(solution)/shard_map/all_to_all | solution.py:396
  24.7 0.1 collective-permute-start
  24.8 1.6 %collective-permute-done.other_ref = f32[800,128]{1,0:T(8,128)S(1)} collective-permute-done((f32[800,128]{1,0:T(8,128)S(1)}, f32[800,128]{1,0:T(8,128)S(1)}, u32[]{:S(2)}, u32[]{:S(2)}) %collective-permute-start) | collective-permute-done | bytes 409632 | tf_op jit(solution)/shard_map/ppermute | solution.py:399
  26.5 8.5 %owner.1 = (f32[32,3136]{1,0:T(8,128)}, f32[256,128]{1,0:T(8,128)S(1)}) custom-call(s32[1]{0:T(128)} %bitcast.parity_ref, f32[800,128]{1,0:T(8,128)S(1)} %bitcast.12, f32[800,128]{1,0:T(8,128)S(1)} %collective-permute-done.other_ref), custom_call_target="tpu_custom_call" | custom-call | tf_op jit(solution)/shard_map/owner/pallas_call | solution.py:401
  35.0 10.3 %all_to_all.11 = f32[32,8,128]{2,1,0:T(8,128)S(1)} all-to-all(f32[32,8,128]{2,1,0:T(8,128)S(1)} %bitcast.13), channel_id=1, replica_groups=mesh['gx'=4,'gy'=8] {'gx','gy'}, dimensions={0} | all-to-all | bytes 262144 | tf_op jit(solution)/shard_map/all_to_all | solution.py:428
  45.2 0.6 %reduce_sum.9 = f32[8,128]{1,0:T(8,128)} reduce(f32[32,8,128]{2,1,0:T(8,128)S(1)} %all_to_all.11, f32[]{:T(128)} %constant.18.clone.1), dimensions={0}, to_apply=%region_0.1 | reduce | flops 31744 | bytes 135172 | tf_op jit(solution)/shard_map/reduce_sum | solution.py:431
Async XLA Ops:
  24.7 1.7 %collective-permute-start = (f32[800,128]{1,0:T(8,128)S(1)}, f32[800,128]{1,0:T(8,128)S(1)}, u32[]{:S(2)}, u32[]{:S(2)}) collective-permute-start(f32[800,128]{1,0:T(8,128)S(1)} %bitcast.11), channel_id=1, source_target_pairs={{0,1},{1,0},{2,3},{3,2},{4,5},{5,4},{6,7},{7,6},{8,9},{9,8},{10,11... | collective-permute-start | bytes 1228808 | tf_op jit(solution)/shard_map/ppermute | solution.py:399

commit v3 on v2

--- a/solution.py
+++ b/solution.py
@@ -17,9 +17,10 @@
 FIELDS = 8
 BLOCK = 448
 SPILL = 64
-ROWS_AT_ONCE = 16
+ROWS_AT_ONCE = 128
 VMEM = pl.BlockSpec(memory_space=pltpu.VMEM)
 SMEM = pl.BlockSpec(memory_space=pltpu.SMEM)
+HBM = pl.BlockSpec(memory_space=pltpu.HBM)
 F32 = jnp.float32
 BF16 = jnp.bfloat16
 
@@ -37,33 +38,68 @@
 
 
 def pack_kernel(
-    devices, count_ref, load_ref, label_ref, coord_ref, charge_ref, shell_ref, atom_ref, slot_ref, out_ref, table_ref
+    devices,
+    load_ref,
+    count_hbm,
+    label_hbm,
+    slot_hbm,
+    atom_hbm,
+    shell_hbm,
+    coord_hbm,
+    charge_hbm,
+    out_ref,
+    count_ref,
+    label_ref,
+    slot_ref,
+    table_ref,
+    shell_ref,
+    coord_ref,
+    charge_ref,
+    sems,
 ):
+    copies = [
+        pltpu.make_async_copy(source, into, sems.at[place])
+        for place, (source, into) in enumerate(
+            (
+                (label_hbm, label_ref),
+                (slot_hbm, slot_ref),
+                (atom_hbm, table_ref.at[0:3, :]),
+                (shell_hbm, shell_ref),
+                (coord_hbm, coord_ref),
+                (charge_hbm, charge_ref),
+                (count_hbm, count_ref),
+            )
+        )
+    ]
+    for copy in copies:
+        copy.start()
     batches, slots = label_ref.shape
     rows = batches * slots
-    atoms = atom_ref.shape[1]
+    atoms = table_ref.shape[1]
     owned = atoms // devices
     per_peer = rows // devices
     halves = charge_ref.shape[1] // LANES
     stride = out_ref.shape[0] // devices
 
-    table_ref[...] = jnp.zeros_like(table_ref)
-    table_ref[0:3, :] = atom_ref[...]
+    for copy in copies[0:3]:
+        copy.wait()
     for tile in range(atoms // LANES):
         table_ref[3:4, tile * LANES : (tile + 1) * LANES] = slot_ref[tile : tile + 1, :].astype(F32)
     label = jnp.concatenate([label_ref[b : b + 1, :] for b in range(batches)], axis=1)
     label = jnp.broadcast_to(label, (8, rows))
     high = lax.shift_right_logical(label, 7)
     low = lax.bitwise_and(label, 127)
+    kept = iota((8, rows), 0) < 4
     found = jnp.zeros((8, rows), F32)
     for tile in range(atoms // LANES):
         piece = table_ref[:, tile * LANES : (tile + 1) * LANES]
         picked = jnp.take_along_axis(piece, low, axis=1, mode="promise_in_bounds")
-        found = jnp.where(high == tile, picked, found)
+        found = jnp.where((high == tile) & kept, picked, found)
     slot = found[3:4, :]
     owner = jnp.floor((slot + 0.5) * (1.0 / owned))
     local = slot - owner * owned
 
+    copies[6].wait()
     lane = iota((1, rows), 1)
     batch_row = jnp.zeros((1, rows), F32)
     live_row = jnp.zeros((1, rows), F32)
@@ -84,6 +120,7 @@
     target = (rank * devices + owner).astype(jnp.int32)
     order = (iota((rows, rows), 0) == target).astype(F32).astype(BF16)
 
+    copies[3].wait()
     shells = shell_ref[...].reshape(rows, halves * LANES).astype(F32).astype(BF16)
     moved = jnp.dot(order, shells, preferred_element_type=F32)
     meta = sum(jnp.dot(order, part, preferred_element_type=F32) for part in three_parts(columns))
@@ -100,6 +137,8 @@
             total = total + (pltpu.roll(piece, FIELDS * c, 1) if c else piece)
         out_ref[pl.ds(base + stride - 1, 8, stride=stride), :] = total
 
+    copies[4].wait()
+    copies[5].wait()
     odd = lax.bitwise_and(iota((8, LANES), 0), 1) == 1
     slot_rank = iota((slots, 1), 0)
     for b in range(batches):
@@ -213,7 +252,7 @@
     copy.start()
 
     sum_ref[...] = jnp.zeros_like(sum_ref)
-    table_ref[...] = jnp.zeros_like(table_ref)
+    table_ref[HARM * pitch :, :] = jnp.zeros(((PAD - HARM) * pitch, LANES), F32)
     for y_ref in (y_own, y_other):
         y_ref[pl.ds(devices * per_peer // 8 * BLOCK, SPILL), :] = jnp.zeros((SPILL, LANES), F32)
 
@@ -280,9 +319,9 @@
     left = iota((owned, LANES), 1) < SHELLS
     row_rank = iota((SHELLS, LANES), 0).astype(F32)
     lane_rank = iota((SHELLS, LANES), 1).astype(F32)
+    lane_rank = jnp.where(lane_rank < SHELLS, lane_rank, lane_rank - SHELLS)
     ratio = jnp.exp(jnp.abs(row_rank - lane_rank) * (-2.3 / SHELLS))
     kernel = jnp.exp(jnp.maximum(row_rank, lane_rank) * (-2.3 / SHELLS)) * 2.0
-    kernel = jnp.where(lane_rank < SHELLS, kernel, 0.0)
     before = None
     for degree in range(LMAX + 1):
         lines = []
@@ -314,8 +353,10 @@
     def split(turn, carry):
         for place in range(8):
             atom = turn * 8 + place
-            both = split_rows(table_ref[pl.ds(atom, PAD, stride=pitch), :])
-            split_ref[pl.ds(pl.multiple_of(atom * 2 * PAD, 16), 2 * PAD), :] = both
+            first, second = two_parts(table_ref[pl.ds(atom, PAD, stride=pitch), :])
+            both = jnp.where(iota((PAD, LANES), 1) < SHELLS, first, second)
+            both = jnp.concatenate([both, jnp.zeros((SHELLS - PAD, LANES), F32)], axis=0)
+            split_ref[pl.ds(pl.multiple_of(atom * SHELLS, SHELLS), SHELLS), :] = both.astype(BF16)
         return carry
 
     lax.fori_loop(0, owned // 8, split, 0)
@@ -324,11 +365,12 @@
         for place in range(step * per_peer):
             source, c = turn * step + place // per_peer, place % per_peer
             local = meta_smem[source, FIELDS * c + 3]
-            table = split_ref[pl.ds(pl.multiple_of(local * 2 * PAD, 16), 2 * PAD), 0:SHELLS]
-            picked = join_rows(jnp.dot(table, hot_shells(source, c), preferred_element_type=F32))
+            table = split_ref[pl.ds(pl.multiple_of(local * SHELLS, SHELLS), SHELLS), :]
+            hot = hot_shells(source, c)
+            picked = jnp.dot(table, jnp.concatenate([hot, hot], axis=0), preferred_element_type=F32)
             at = ((source // 8) * per_peer + c) * 72 + source % 8
             for side, (y_ref, part_ref) in enumerate(((y_own, part_own), (y_other, part_other))):
-                product = picked[:, side * LANES : (side + 1) * LANES] * harmonic_rows(source, c, y_ref)
+                product = picked[0:PAD, side * LANES : (side + 1) * LANES] * harmonic_rows(source, c, y_ref)
                 part_ref[pl.ds(at, 8, stride=9), :] = jnp.sum(product.reshape(PAD // 8, 8, LANES), axis=0)
         return carry
 
@@ -379,19 +421,34 @@
     outgoing = pl.pallas_call(
         functools.partial(pack_kernel, devices),
         out_shape=jax.ShapeDtypeStruct((devices * stride, LANES), F32),
-        in_specs=[SMEM, SMEM] + [VMEM] * 6,
+        in_specs=[SMEM] + [HBM] * 7,
         out_specs=VMEM,
-        scratch_shapes=[pltpu.VMEM((8, atoms), F32)],
+        scratch_shapes=[
+            pltpu.SMEM((batches,), jnp.int32),
+            pltpu.VMEM((batches, slots), jnp.int32),
+            pltpu.VMEM((atoms // LANES, LANES), jnp.int32),
+            pltpu.VMEM((8, atoms), F32),
+            pltpu.VMEM((batches, slots, points), jnp.int32),
+            pltpu.VMEM((3, batches, points), F32),
+            pltpu.VMEM((batches, points), F32),
+            pltpu.SemaphoreType.DMA((7,)),
+        ],
+        compiler_params=pltpu.CompilerParams(vmem_limit_bytes=16 << 20),
         name="pack",
     )(
-        neighbour_count,
         batch_load,
-        neighbours,
-        jnp.transpose(point_coords, (1, 0, 2)),
-        charge,
-        shell_index,
-        atom_coords,
-        owner_slot.reshape(atoms // LANES, LANES),
+        *(
+            pltpu.with_memory_space_constraint(value, pltpu.HBM)
+            for value in (
+                neighbour_count,
+                neighbours,
+                owner_slot.reshape(atoms // LANES, LANES),
+                atom_coords,
+                shell_index,
+                jnp.transpose(point_coords, (1, 0, 2)),
+                charge,
+            )
+        ),
     )
     arrived = lax.all_to_all(
         outgoing.reshape(devices, stride, 1, LANES), ("gx", "gy"), split_axis=0, concat_axis=0, tiled=True
@@ -405,7 +462,7 @@
             jax.ShapeDtypeStruct((devices * 2 * batches, LANES), F32),
         ),
         in_specs=[SMEM, VMEM, VMEM],
-        out_specs=(pl.BlockSpec(memory_space=pltpu.HBM), VMEM),
+        out_specs=(HBM, VMEM),
         scratch_shapes=[
             pltpu.VMEM((rows // 8 * BLOCK + SPILL, LANES), F32),
             pltpu.VMEM((rows // 8 * BLOCK + SPILL, LANES), F32),
@@ -413,7 +470,7 @@
             pltpu.VMEM((rows, LANES), F32),
             pltpu.VMEM((PAD * (owned + 1), LANES), F32),
             pltpu.VMEM((PAD * (owned + 1), LANES), F32),
-            pltpu.VMEM((owned * 2 * PAD, LANES), BF16),
+            pltpu.VMEM((owned * SHELLS, LANES), BF16),
             pltpu.VMEM((rows * 9, LANES), F32),
             pltpu.VMEM((rows * 9, LANES), F32),
             pltpu.VMEM((owned, HARM * SHELLS), F32),

time: 46.1 us -> 42.2 us (0.915)
  Pallas kernels: 10.8 us -> 7.1 us
    pallas_call x1, Pallas kernels: 8.5 us -> 5.5 us  [body(): pl.pallas_call(functools.partial(owner_kernel, devices, per_peer, batches...]
    pallas_call x1, Pallas kernels: 2.32 us -> 1.6 us  [body(): pl.pallas_call(functools.partial(pack_kernel, devices), out_shape=jax.Sha...]
where the time goes in v3:
time: 42.2 us; the launch traced here: 42 us
  blocking collectives  31.2 us (74%)
  Pallas kernels  7.1 us (17%)
  waiting for transfers between devices  1.63 us (4%)
  between operations  1.3 us (3%)
  other arithmetic  0.63 us (1%)
    all_to_all x1, blocking collectives, body(): lax.all_to_all(outgoing.reshape(devices, stride, 1, LANES), ('gx', 'gy'),...  20.9 us
    all_to_all x1, blocking collectives, body(): lax.all_to_all(reply.reshape(devices, 2 * batches, LANES), ('gx', 'gy'),...  10.3 us
    pallas_call x1, Pallas kernels, body(): pl.pallas_call(functools.partial(owner_kernel, devices, per_peer, batches...  5.5 us
    ppermute x1, waiting for transfers between devices, body(): swapped = lax.ppermute(arrived, 'gy', [(i, i ^ 1) for i in range(count_gy)])  1.63 us
    pallas_call x1, Pallas kernels, body(): pl.pallas_call(functools.partial(pack_kernel, devices), out_shape=jax.Sha...  1.6 us
  transfers between devices with their start and end apart: 1, of which 1 were waited for; matrix products, arithmetic and copies ran while one was open for 0% of the time, Pallas kernels for 0%

profile of v3, /device:TPU:0, one launch (start us, length us, event | category | flops | bytes accessed | tf_op | source)
XLA Modules:
  0.0 42.0 jit_solution(6782736982187584136)
XLA Ops:
  1.3 1.6 %pack.1 = f32[800,128]{1,0:T(8,128)S(1)} custom-call(s32[1]{0:T(128)S(6)} %copy.11.load_ref, s32[4]{0:T(128)} %count_hbm.1, s32[4,32]{1,0:T(4,128)} %label_hbm.1, s32[8,128]{1,0:T(8,128)} %bitcast.16, f32[3,1024]{1,0:T(4,128)} %atom_hbm.1, s32[4,32,256]{2,1,0:T(8,128)} %shell_hbm.1, f32[3,4,256]{2,1,0:T(4,128)} %bitcast.15, f32[4,256]{1,0:T(4,128)} %charge_hbm.1), custom_call_target="tpu_custom_call" | custom-call | tf_op jit(solution)/shard_map/pack/pallas_call | solution.py:421
  2.9 20.9 %all_to_all.10 = f32[32,25,1,128]{3,2,1,0:T(1,128)S(1)} all-to-all(f32[32,25,1,128]{3,2,1,0:T(1,128)S(1)} %bitcast.13), channel_id=1, replica_groups=mesh['gx'=4,'gy'=8] {'gx','gy'}, dimensions={0} | all-to-all | bytes 819200 | tf_op jit(solution)/shard_map/all_to_all | solution.py:453
  23.8 0.1 collective-permute-start
  23.9 1.6 %collective-permute-done.other_ref = f32[800,128]{1,0:T(8,128)S(1)} collective-permute-done((f32[800,128]{1,0:T(8,128)S(1)}, f32[800,128]{1,0:T(8,128)S(1)}, u32[]{:S(2)}, u32[]{:S(2)}) %collective-permute-start) | collective-permute-done | bytes 409632 | tf_op jit(solution)/shard_map/ppermute | solution.py:456
  25.5 5.5 %owner.1 = (f32[32,3136]{1,0:T(8,128)}, f32[256,128]{1,0:T(8,128)S(1)}) custom-call(s32[1]{0:T(128)} %bitcast.parity_ref, f32[800,128]{1,0:T(8,128)S(1)} %bitcast.12, f32[800,128]{1,0:T(8,128)S(1)} %collective-permute-done.other_ref), custom_call_target="tpu_custom_call" | custom-call | tf_op jit(solution)/shard_map/owner/pallas_call | solution.py:458
  31.1 10.3 %all_to_all.11 = f32[32,8,128]{2,1,0:T(8,128)S(1)} all-to-all(f32[32,8,128]{2,1,0:T(8,128)S(1)} %bitcast.14), channel_id=1, replica_groups=mesh['gx'=4,'gy'=8] {'gx','gy'}, dimensions={0} | all-to-all | bytes 262144 | tf_op jit(solution)/shard_map/all_to_all | solution.py:485
  41.3 0.6 %reduce_sum.9 = f32[8,128]{1,0:T(8,128)} reduce(f32[32,8,128]{2,1,0:T(8,128)S(1)} %all_to_all.11, f32[]{:T(128)} %constant.18.clone.1), dimensions={0}, to_apply=%region_0.1 | reduce | flops 31744 | bytes 135172 | tf_op jit(solution)/shard_map/reduce_sum | solution.py:488
Async XLA Ops:
  23.8 1.7 %collective-permute-start = (f32[800,128]{1,0:T(8,128)S(1)}, f32[800,128]{1,0:T(8,128)S(1)}, u32[]{:S(2)}, u32[]{:S(2)}) collective-permute-start(f32[800,128]{1,0:T(8,128)S(1)} %bitcast.11), channel_id=1, source_target_pairs={{0,1},{1,0},{2,3},{3,2},{4,5},{5,4},{6,7},{7,6},{8,9},{9,8},{10,11... | collective-permute-start | bytes 1228808 | tf_op jit(solution)/shard_map/ppermute | solution.py:456

commit v4 on v3

--- a/solution.py
+++ b/solution.py
@@ -99,7 +99,8 @@
     owner = jnp.floor((slot + 0.5) * (1.0 / owned))
     local = slot - owner * owned
 
-    copies[6].wait()
+    for copy in copies[3:]:
+        copy.wait()
     lane = iota((1, rows), 1)
     batch_row = jnp.zeros((1, rows), F32)
     live_row = jnp.zeros((1, rows), F32)
@@ -120,7 +121,6 @@
     target = (rank * devices + owner).astype(jnp.int32)
     order = (iota((rows, rows), 0) == target).astype(F32).astype(BF16)
 
-    copies[3].wait()
     shells = shell_ref[...].reshape(rows, halves * LANES).astype(F32).astype(BF16)
     moved = jnp.dot(order, shells, preferred_element_type=F32)
     meta = sum(jnp.dot(order, part, preferred_element_type=F32) for part in three_parts(columns))
@@ -137,8 +137,6 @@
             total = total + (pltpu.roll(piece, FIELDS * c, 1) if c else piece)
         out_ref[pl.ds(base + stride - 1, 8, stride=stride), :] = total
 
-    copies[4].wait()
-    copies[5].wait()
     odd = lax.bitwise_and(iota((8, LANES), 0), 1) == 1
     slot_rank = iota((slots, 1), 0)
     for b in range(batches):
@@ -209,6 +207,45 @@
     return first, value - first
 
 
+def column(line, c, field):
+    at = FIELDS * c + field
+    return jnp.broadcast_to(line[:, at : at + 1], (8, LANES))
+
+
+def geometry(devices, per_peer, batches, own_ref, source, y_ref, w_ref):
+    stride = own_ref.shape[0] // devices
+    shell_rows = per_peer * 2
+    y_ref[pl.ds(devices * per_peer // 8 * BLOCK, SPILL), :] = jnp.zeros((SPILL, LANES), F32)
+
+    def one(group, carry):
+        base = group * 8 * stride
+        line = own_ref[pl.ds(base + stride - 1, 8, stride=stride), :]
+        points = [
+            [source[pl.ds(base + shell_rows + b * 4 + i, 8, stride=stride), :] for i in range(4)]
+            for b in range(batches)
+        ]
+        for c in range(per_peer):
+            batch = column(line, c, 4)
+            chosen = list(points[0])
+            for b in range(1, batches):
+                chosen = [jnp.where(batch == b, new, old) for new, old in zip(points[b], chosen)]
+            offset = [chosen[i] - column(line, c, i) for i in range(3)]
+            squared = offset[0] * offset[0] + offset[1] * offset[1] + offset[2] * offset[2]
+            scale = lax.rsqrt(squared + SOFTEN)
+            weight = jnp.where(column(line, c, 5) > 0.5, chosen[3] / (1.0 + squared), 0.0)
+            w_ref[pl.ds(group * 8 * per_peer + c, 8, stride=per_peer), :] = weight
+            start = pl.multiple_of((group * per_peer + c) * BLOCK, 8)
+            for k, value in harmonics(*(part * scale for part in offset)):
+                y_ref[pl.ds(start + k * 9, 8), :] = jnp.broadcast_to(value, (8, LANES))
+        return carry
+
+    lax.fori_loop(0, devices // 8, one, 0)
+
+
+def own_kernel(devices, per_peer, batches, own_ref, y_ref, w_ref):
+    geometry(devices, per_peer, batches, own_ref, own_ref, y_ref, w_ref)
+
+
 def owner_kernel(
     devices,
     per_peer,
@@ -216,11 +253,11 @@
     parity_ref,
     own_ref,
     other_ref,
+    y_own,
+    w_own,
     moment_hbm,
     reply_ref,
-    y_own,
     y_other,
-    w_own,
     w_other,
     sum_ref,
     table_ref,
@@ -237,7 +274,6 @@
     groups = devices // 8
     owned = moment_ref.shape[0]
     pitch = owned + 1
-    shell_rows = per_peer * 2
     parity = parity_ref[0]
     step = max(1, ROWS_AT_ONCE // per_peer)
 
@@ -253,37 +289,8 @@
 
     sum_ref[...] = jnp.zeros_like(sum_ref)
     table_ref[HARM * pitch :, :] = jnp.zeros(((PAD - HARM) * pitch, LANES), F32)
-    for y_ref in (y_own, y_other):
-        y_ref[pl.ds(devices * per_peer // 8 * BLOCK, SPILL), :] = jnp.zeros((SPILL, LANES), F32)
-
-    def column(line, c, field):
-        at = FIELDS * c + field
-        return jnp.broadcast_to(line[:, at : at + 1], (8, LANES))
-
-    def geometry(group, carry):
-        base = group * 8 * stride
-        line = own_ref[pl.ds(base + stride - 1, 8, stride=stride), :]
-        for source, y_ref, w_ref in ((own_ref, y_own, w_own), (other_ref, y_other, w_other)):
-            points = [
-                [source[pl.ds(base + shell_rows + b * 4 + i, 8, stride=stride), :] for i in range(4)]
-                for b in range(batches)
-            ]
-            for c in range(per_peer):
-                batch = column(line, c, 4)
-                chosen = list(points[0])
-                for b in range(1, batches):
-                    chosen = [jnp.where(batch == b, new, old) for new, old in zip(points[b], chosen)]
-                offset = [chosen[i] - column(line, c, i) for i in range(3)]
-                squared = offset[0] * offset[0] + offset[1] * offset[1] + offset[2] * offset[2]
-                scale = lax.rsqrt(squared + SOFTEN)
-                weight = jnp.where(column(line, c, 5) > 0.5, chosen[3] / (1.0 + squared), 0.0)
-                w_ref[pl.ds(group * 8 * per_peer + c, 8, stride=per_peer), :] = weight
-                start = pl.multiple_of((group * per_peer + c) * BLOCK, 8)
-                for k, value in harmonics(*(part * scale for part in offset)):
-                    y_ref[pl.ds(start + k * 9, 8), :] = jnp.broadcast_to(value, (8, LANES))
-        return carry
-
-    lax.fori_loop(0, groups, geometry, 0)
+
+    geometry(devices, per_peer, batches, own_ref, other_ref, y_other, w_other)
     copy.wait()
 
     def hot_shells(source, c):
@@ -327,24 +334,21 @@
         lines = []
         for k in range(degree * degree, (degree + 1) ** 2):
             line = sum_ref[k * pitch : k * pitch + owned, :]
+            line = line + pltpu.roll(line, SHELLS, 1)
             lines.append(line)
-            if k % 2 == 0:
+            if k == HARM - 1:
+                moment_ref[:, k * SHELLS : (k + 1) * SHELLS] = line[:, 0:SHELLS]
+            elif k % 2 == 0:
                 before = line
-                if k == HARM - 1:
-                    moment_ref[:, k * SHELLS : (k + 1) * SHELLS] = line[:, 0:SHELLS]
             else:
-                moment_ref[:, (k - 1) * SHELLS : (k + 1) * SHELLS] = jnp.where(
-                    left, before, pltpu.roll(line, SHELLS, 1)
-                )
+                moment_ref[:, (k - 1) * SHELLS : (k + 1) * SHELLS] = jnp.where(left, before, line)
         green = kernel * (4.0 * math.pi / (2 * degree + 1))
         kernel = kernel * ratio
-        g_first, g_second = two_parts(green)
+        green = jnp.concatenate(two_parts(green), axis=1).astype(BF16)
         first, second = two_parts(jnp.concatenate(lines, axis=0))
-        both = (first + pltpu.roll(second, SHELLS, 1)).astype(BF16)
-        made = jnp.dot(both, jnp.concatenate([g_first, g_first], axis=0).astype(BF16), preferred_element_type=F32)
-        made = made + jnp.dot(
-            both, jnp.concatenate([g_second, g_second], axis=0).astype(BF16), preferred_element_type=F32
-        )
+        both = jnp.where(iota(first.shape, 1) < SHELLS, first, second).astype(BF16)
+        made = jnp.dot(both, jnp.concatenate([green, green], axis=0), preferred_element_type=F32)
+        made = made[:, 0:LANES] + made[:, LANES : 2 * LANES]
         for place, k in enumerate(range(degree * degree, (degree + 1) ** 2)):
             table_ref[k * pitch : k * pitch + owned, :] = made[place * owned : (place + 1) * owned, :]
     result = pltpu.make_async_copy(moment_ref, moment_hbm, out_sem)
@@ -455,18 +459,26 @@
     ).reshape(devices * stride, LANES)
     swapped = lax.ppermute(arrived, "gy", [(i, i ^ 1) for i in range(count_gy)])
     parity = (lax.axis_index("gy") % 2).astype(jnp.int32).reshape(1)
+    held = rows // 8 * BLOCK + SPILL
+    y_own, w_own = pl.pallas_call(
+        functools.partial(own_kernel, devices, per_peer, batches),
+        out_shape=(jax.ShapeDtypeStruct((held, LANES), F32), jax.ShapeDtypeStruct((rows, LANES), F32)),
+        in_specs=[VMEM],
+        out_specs=(VMEM, VMEM),
+        compiler_params=pltpu.CompilerParams(vmem_limit_bytes=24 << 20),
+        cost_estimate=pl.CostEstimate(flops=2_000_000_000, bytes_accessed=1000, transcendentals=0),
+        name="own",
+    )(arrived)
     moments, reply = pl.pallas_call(
         functools.partial(owner_kernel, devices, per_peer, batches),
         out_shape=(
             jax.ShapeDtypeStruct((owned, HARM * SHELLS), F32),
             jax.ShapeDtypeStruct((devices * 2 * batches, LANES), F32),
         ),
-        in_specs=[SMEM, VMEM, VMEM],
+        in_specs=[SMEM] + [VMEM] * 4,
         out_specs=(HBM, VMEM),
         scratch_shapes=[
-            pltpu.VMEM((rows // 8 * BLOCK + SPILL, LANES), F32),
-            pltpu.VMEM((rows // 8 * BLOCK + SPILL, LANES), F32),
-            pltpu.VMEM((rows, LANES), F32),
+            pltpu.VMEM((held, LANES), F32),
             pltpu.VMEM((rows, LANES), F32),
             pltpu.VMEM((PAD * (owned + 1), LANES), F32),
             pltpu.VMEM((PAD * (owned + 1), LANES), F32),
@@ -481,7 +493,7 @@
         ],
         compiler_params=pltpu.CompilerParams(vmem_limit_bytes=24 << 20),
         name="owner",
-    )(parity, arrived, swapped)
+    )(parity, arrived, swapped, y_own, w_own)
     returned = lax.all_to_all(
         reply.reshape(devices, 2 * batches, LANES), ("gx", "gy"), split_axis=0, concat_axis=0, tiled=True
     )

time: 42.2 us -> 41.7 us (0.988)
  waiting for transfers between devices: 1.63 us -> 0.92 us
    ppermute x1, waiting for transfers between devices: 1.63 us -> 0.92 us  [body(): swapped = lax.ppermute(arrived, 'gy', [(i, i ^ 1) for i in range(count_gy)])]
    pallas_call x0 -> x1, Pallas kernels: none -> 0.7 us  [body(): pl.pallas_call(functools.partial(own_kernel, devices, per_peer, batches),...]
  transfers between devices with their start and end apart: 1 -> 1, of which waited for: 1 -> 1; matrix products, arithmetic and copies ran while one was open for 0% -> 0% of each run, Pallas kernels for 0% -> 2%
where the time goes in v4:
time: 41.7 us; the launch traced here: 41.5 us
  blocking collectives  31.2 us (75%)
  Pallas kernels  7.4 us (18%)
  between operations  1.3 us (3%)
  waiting for transfers between devices  0.92 us (2%)
  other arithmetic  0.63 us (2%)
    all_to_all x1, blocking collectives, body(): lax.all_to_all(outgoing.reshape(devices, stride, 1, LANES), ('gx', 'gy'),...  20.9 us
    all_to_all x1, blocking collectives, body(): lax.all_to_all(reply.reshape(devices, 2 * batches, LANES), ('gx', 'gy'),...  10.3 us
    pallas_call x1, Pallas kernels, body(): pl.pallas_call(functools.partial(owner_kernel, devices, per_peer, batches...  5.19 us
    pallas_call x1, Pallas kernels, body(): pl.pallas_call(functools.partial(pack_kernel, devices), out_shape=jax.Sha...  1.51 us
    ppermute x1, waiting for transfers between devices, body(): swapped = lax.ppermute(arrived, 'gy', [(i, i ^ 1) for i in range(count_gy)])  0.92 us
  transfers between devices with their start and end apart: 1, of which 1 were waited for; matrix products, arithmetic and copies ran while one was open for 0% of the time, Pallas kernels for 2%

profile of v4, /device:TPU:0, one launch (start us, length us, event | category | flops | bytes accessed | tf_op | source)
XLA Modules:
  0.0 41.5 jit_solution(9322372076037900264)
XLA Ops:
  1.3 1.5 %pack.1 = f32[800,128]{1,0:T(8,128)S(1)} custom-call(s32[1]{0:T(128)S(6)} %copy.11.load_ref, s32[4]{0:T(128)} %count_hbm.1, s32[4,32]{1,0:T(4,128)} %label_hbm.1, s32[8,128]{1,0:T(8,128)} %bitcast.17, f32[3,1024]{1,0:T(4,128)} %atom_hbm.1, s32[4,32,256]{2,1,0:T(8,128)} %shell_hbm.1, f32[3,4,256]{2,1,0:T(4,128)} %bitcast.16, f32[4,256]{1,0:T(4,128)} %charge_hbm.1), custom_call_target="tpu_custom_call" | custom-call | tf_op jit(solution)/shard_map/pack/pallas_call | solution.py:425
  2.8 20.9 %all_to_all.10 = f32[32,25,1,128]{3,2,1,0:T(1,128)S(1)} all-to-all(f32[32,25,1,128]{3,2,1,0:T(1,128)S(1)} %bitcast.14), channel_id=1, replica_groups=mesh['gx'=4,'gy'=8] {'gx','gy'}, dimensions={0} | all-to-all | bytes 819200 | tf_op jit(solution)/shard_map/all_to_all | solution.py:457
  23.7 0.1 collective-permute-start
  23.8 0.7 %own.1 = (f32[7232,128]{1,0:T(8,128)S(1)}, f32[128,128]{1,0:T(8,128)S(1)}) custom-call(f32[800,128]{1,0:T(8,128)S(1)} %bitcast.12), custom_call_target="tpu_custom_call" | custom-call | flops 2000000000 | bytes 1000 | tf_op jit(solution)/shard_map/own/pallas_call | solution.py:463
  24.5 0.9 %collective-permute-done.other_ref = f32[800,128]{1,0:T(8,128)S(1)} collective-permute-done((f32[800,128]{1,0:T(8,128)S(1)}, f32[800,128]{1,0:T(8,128)S(1)}, u32[]{:S(2)}, u32[]{:S(2)}) %collective-permute-start) | collective-permute-done | bytes 409632 | tf_op jit(solution)/shard_map/ppermute | solution.py:460
  25.5 5.2 %owner.1 = (f32[32,3136]{1,0:T(8,128)}, f32[256,128]{1,0:T(8,128)S(1)}) custom-call(s32[1]{0:T(128)} %bitcast.parity_ref, f32[800,128]{1,0:T(8,128)S(1)} %bitcast.13, f32[800,128]{1,0:T(8,128)S(1)} %collective-permute-done.other_ref, f32[7232,128]{1,0:T(8,128)S(1)} %get-tuple-element.6.y_own, f32[128,128]{1,0:T(8,128)S(1)} %get-tuple-element.7.w_own), custom_call_target="tpu_custom_call" | custom-call | tf_op jit(solution)/shard_map/owner/pallas_call | solution.py:472
  30.6 10.3 %all_to_all.11 = f32[32,8,128]{2,1,0:T(8,128)S(1)} all-to-all(f32[32,8,128]{2,1,0:T(8,128)S(1)} %bitcast.15), channel_id=1, replica_groups=mesh['gx'=4,'gy'=8] {'gx','gy'}, dimensions={0} | all-to-all | bytes 262144 | tf_op jit(solution)/shard_map/all_to_all | solution.py:497
  40.9 0.6 %reduce_sum.9 = f32[8,128]{1,0:T(8,128)} reduce(f32[32,8,128]{2,1,0:T(8,128)S(1)} %all_to_all.11, f32[]{:T(128)} %constant.18.clone.1), dimensions={0}, to_apply=%region_0.1 | reduce | flops 31744 | bytes 135172 | tf_op jit(solution)/shard_map/reduce_sum | solution.py:500
Async XLA Ops:
  23.7 1.7 %collective-permute-start = (f32[800,128]{1,0:T(8,128)S(1)}, f32[800,128]{1,0:T(8,128)S(1)}, u32[]{:S(2)}, u32[]{:S(2)}) collective-permute-start(f32[800,128]{1,0:T(8,128)S(1)} %bitcast.11), channel_id=1, source_target_pairs={{0,1},{1,0},{2,3},{3,2},{4,5},{5,4},{6,7},{7,6},{8,9},{9,8},{10,11... | collective-permute-start | bytes 1228808 | tf_op jit(solution)/shard_map/ppermute | solution.py:460

commit v5 on v4

--- a/solution.py
+++ b/solution.py
@@ -375,7 +375,9 @@
             at = ((source // 8) * per_peer + c) * 72 + source % 8
             for side, (y_ref, part_ref) in enumerate(((y_own, part_own), (y_other, part_other))):
                 product = picked[0:PAD, side * LANES : (side + 1) * LANES] * harmonic_rows(source, c, y_ref)
-                part_ref[pl.ds(at, 8, stride=9), :] = jnp.sum(product.reshape(PAD // 8, 8, LANES), axis=0)
+                main = jnp.sum(product[0 : PAD - 8].reshape(PAD // 8 - 1, 8, LANES), axis=0)
+                last = jnp.where(iota((8, LANES), 0) < HARM - (PAD - 8), product[PAD - 8 :], 0.0)
+                part_ref[pl.ds(at, 8, stride=9), :] = main + last
         return carry
 
     lax.fori_loop(0, devices // step, evaluate, 0)

time: 41.7 us -> 41.7 us (level)
  no operation moved by 1% of the time
where the time goes in v5:
time: 41.7 us; the launch traced here: 41.5 us
  blocking collectives  31.2 us (75%)
  Pallas kernels  7.39 us (18%)
  between operations  1.3 us (3%)
  waiting for transfers between devices  0.92 us (2%)
  other arithmetic  0.63 us (2%)
    all_to_all x1, blocking collectives, body(): lax.all_to_all(outgoing.reshape(devices, stride, 1, LANES), ('gx', 'gy'),...  20.9 us
    all_to_all x1, blocking collectives, body(): lax.all_to_all(reply.reshape(devices, 2 * batches, LANES), ('gx', 'gy'),...  10.3 us
    pallas_call x1, Pallas kernels, body(): pl.pallas_call(functools.partial(owner_kernel, devices, per_peer, batches...  5.18 us
    pallas_call x1, Pallas kernels, body(): pl.pallas_call(functools.partial(pack_kernel, devices), out_shape=jax.Sha...  1.51 us
    ppermute x1, waiting for transfers between devices, body(): swapped = lax.ppermute(arrived, 'gy', [(i, i ^ 1) for i in range(count_gy)])  0.92 us
  transfers between devices with their start and end apart: 1, of which 1 were waited for; matrix products, arithmetic and copies ran while one was open for 0% of the time, Pallas kernels for 2%

profile of v5, /device:TPU:0, one launch (start us, length us, event | category | flops | bytes accessed | tf_op | source)
XLA Modules:
  0.0 41.5 jit_solution(3456482253217902654)
XLA Ops:
  1.3 1.5 %pack.1 = f32[800,128]{1,0:T(8,128)S(1)} custom-call(s32[1]{0:T(128)S(6)} %copy.11.load_ref, s32[4]{0:T(128)} %count_hbm.1, s32[4,32]{1,0:T(4,128)} %label_hbm.1, s32[8,128]{1,0:T(8,128)} %bitcast.17, f32[3,1024]{1,0:T(4,128)} %atom_hbm.1, s32[4,32,256]{2,1,0:T(8,128)} %shell_hbm.1, f32[3,4,256]{2,1,0:T(4,128)} %bitcast.16, f32[4,256]{1,0:T(4,128)} %charge_hbm.1), custom_call_target="tpu_custom_call" | custom-call | tf_op jit(solution)/shard_map/pack/pallas_call | solution.py:427
  2.8 20.9 %all_to_all.10 = f32[32,25,1,128]{3,2,1,0:T(1,128)S(1)} all-to-all(f32[32,25,1,128]{3,2,1,0:T(1,128)S(1)} %bitcast.14), channel_id=1, replica_groups=mesh['gx'=4,'gy'=8] {'gx','gy'}, dimensions={0} | all-to-all | bytes 819200 | tf_op jit(solution)/shard_map/all_to_all | solution.py:459
  23.7 0.1 collective-permute-start
  23.8 0.7 %own.1 = (f32[7232,128]{1,0:T(8,128)S(1)}, f32[128,128]{1,0:T(8,128)S(1)}) custom-call(f32[800,128]{1,0:T(8,128)S(1)} %bitcast.12), custom_call_target="tpu_custom_call" | custom-call | flops 2000000000 | bytes 1000 | tf_op jit(solution)/shard_map/own/pallas_call | solution.py:465
  24.5 0.9 %collective-permute-done.other_ref = f32[800,128]{1,0:T(8,128)S(1)} collective-permute-done((f32[800,128]{1,0:T(8,128)S(1)}, f32[800,128]{1,0:T(8,128)S(1)}, u32[]{:S(2)}, u32[]{:S(2)}) %collective-permute-start) | collective-permute-done | bytes 409632 | tf_op jit(solution)/shard_map/ppermute | solution.py:462
  25.5 5.2 %owner.1 = (f32[32,3136]{1,0:T(8,128)}, f32[256,128]{1,0:T(8,128)S(1)}) custom-call(s32[1]{0:T(128)} %bitcast.parity_ref, f32[800,128]{1,0:T(8,128)S(1)} %bitcast.13, f32[800,128]{1,0:T(8,128)S(1)} %collective-permute-done.other_ref, f32[7232,128]{1,0:T(8,128)S(1)} %get-tuple-element.6.y_own, f32[128,128]{1,0:T(8,128)S(1)} %get-tuple-element.7.w_own), custom_call_target="tpu_custom_call" | custom-call | tf_op jit(solution)/shard_map/owner/pallas_call | solution.py:474
  30.6 10.3 %all_to_all.11 = f32[32,8,128]{2,1,0:T(8,128)S(1)} all-to-all(f32[32,8,128]{2,1,0:T(8,128)S(1)} %bitcast.15), channel_id=1, replica_groups=mesh['gx'=4,'gy'=8] {'gx','gy'}, dimensions={0} | all-to-all | bytes 262144 | tf_op jit(solution)/shard_map/all_to_all | solution.py:499
  40.9 0.6 %reduce_sum.9 = f32[8,128]{1,0:T(8,128)} reduce(f32[32,8,128]{2,1,0:T(8,128)S(1)} %all_to_all.11, f32[]{:T(128)} %constant.18.clone.1), dimensions={0}, to_apply=%region_0.1 | reduce | flops 31744 | bytes 135172 | tf_op jit(solution)/shard_map/reduce_sum | solution.py:502
Async XLA Ops:
  23.7 1.7 %collective-permute-start = (f32[800,128]{1,0:T(8,128)S(1)}, f32[800,128]{1,0:T(8,128)S(1)}, u32[]{:S(2)}, u32[]{:S(2)}) collective-permute-start(f32[800,128]{1,0:T(8,128)S(1)} %bitcast.11), channel_id=1, source_target_pairs={{0,1},{1,0},{2,3},{3,2},{4,5},{5,4},{6,7},{7,6},{8,9},{9,8},{10,11... | collective-permute-start | bytes 1228808 | tf_op jit(solution)/shard_map/ppermute | solution.py:462

commit v6 on v5

--- a/solution.py
+++ b/solution.py
@@ -242,7 +242,11 @@
     lax.fori_loop(0, devices // 8, one, 0)
 
 
-def own_kernel(devices, per_peer, batches, own_ref, y_ref, w_ref):
+def own_kernel(devices, per_peer, batches, own_ref, y_ref, w_ref, meta_ref):
+    stride = own_ref.shape[0] // devices
+    for group in range(devices // 8):
+        line = own_ref[pl.ds(group * 8 * stride + stride - 1, 8, stride=stride), :]
+        meta_ref[group * 8 : group * 8 + 8, :] = line.astype(jnp.int32)
     geometry(devices, per_peer, batches, own_ref, own_ref, y_ref, w_ref)
 
 
@@ -255,6 +259,7 @@
     other_ref,
     y_own,
     w_own,
+    meta_ref,
     moment_hbm,
     reply_ref,
     y_other,
@@ -265,7 +270,6 @@
     part_own,
     part_other,
     moment_ref,
-    meta_ref,
     meta_smem,
     sem,
     out_sem,
@@ -277,13 +281,6 @@
     parity = parity_ref[0]
     step = max(1, ROWS_AT_ONCE // per_peer)
 
-    def gather_meta(group, carry):
-        at = pl.multiple_of(group * 8, 8)
-        line = own_ref[pl.ds(group * 8 * stride + stride - 1, 8, stride=stride), :]
-        meta_ref[pl.ds(at, 8), :] = line.astype(jnp.int32)
-        return carry
-
-    lax.fori_loop(0, groups, gather_meta, 0)
     copy = pltpu.make_async_copy(meta_ref, meta_smem, sem)
     copy.start()
 
@@ -462,11 +459,15 @@
     swapped = lax.ppermute(arrived, "gy", [(i, i ^ 1) for i in range(count_gy)])
     parity = (lax.axis_index("gy") % 2).astype(jnp.int32).reshape(1)
     held = rows // 8 * BLOCK + SPILL
-    y_own, w_own = pl.pallas_call(
+    y_own, w_own, meta = pl.pallas_call(
         functools.partial(own_kernel, devices, per_peer, batches),
-        out_shape=(jax.ShapeDtypeStruct((held, LANES), F32), jax.ShapeDtypeStruct((rows, LANES), F32)),
+        out_shape=(
+            jax.ShapeDtypeStruct((held, LANES), F32),
+            jax.ShapeDtypeStruct((rows, LANES), F32),
+            jax.ShapeDtypeStruct((devices, LANES), jnp.int32),
+        ),
         in_specs=[VMEM],
-        out_specs=(VMEM, VMEM),
+        out_specs=(VMEM, VMEM, VMEM),
         compiler_params=pltpu.CompilerParams(vmem_limit_bytes=24 << 20),
         cost_estimate=pl.CostEstimate(flops=2_000_000_000, bytes_accessed=1000, transcendentals=0),
         name="own",
@@ -477,7 +478,7 @@
             jax.ShapeDtypeStruct((owned, HARM * SHELLS), F32),
             jax.ShapeDtypeStruct((devices * 2 * batches, LANES), F32),
         ),
-        in_specs=[SMEM] + [VMEM] * 4,
+        in_specs=[SMEM] + [VMEM] * 5,
         out_specs=(HBM, VMEM),
         scratch_shapes=[
             pltpu.VMEM((held, LANES), F32),
@@ -488,17 +489,16 @@
             pltpu.VMEM((rows * 9, LANES), F32),
             pltpu.VMEM((rows * 9, LANES), F32),
             pltpu.VMEM((owned, HARM * SHELLS), F32),
-            pltpu.VMEM((devices, LANES), jnp.int32),
             pltpu.SMEM((devices, LANES), jnp.int32),
             pltpu.SemaphoreType.DMA,
             pltpu.SemaphoreType.DMA,
         ],
         compiler_params=pltpu.CompilerParams(vmem_limit_bytes=24 << 20),
         name="owner",
-    )(parity, arrived, swapped, y_own, w_own)
+    )(parity, arrived, swapped, y_own, w_own, meta)
     returned = lax.all_to_all(
-        reply.reshape(devices, 2 * batches, LANES), ("gx", "gy"), split_axis=0, concat_axis=0, tiled=True
-    )
+        reply.reshape(devices, 2 * batches, 1, LANES), ("gx", "gy"), split_axis=0, concat_axis=0, tiled=True
+    ).reshape(devices, 2 * batches, LANES)
     potential = jnp.sum(returned, axis=0).reshape(2, batches, LANES)
     return jnp.transpose(potential, (1, 0, 2)).reshape(batches, points), moments
 

time: 41.7 us -> 41.7 us (level)
  no operation moved by 1% of the time
where the time goes in v6:
time: 41.7 us; the launch traced here: 41.5 us
  blocking collectives  31.2 us (75%)
  Pallas kernels  7.39 us (18%)
  between operations  1.3 us (3%)
  waiting for transfers between devices  0.92 us (2%)
  other arithmetic  0.63 us (2%)
    all_to_all x1, blocking collectives, body(): lax.all_to_all(outgoing.reshape(devices, stride, 1, LANES), ('gx', 'gy'),...  20.9 us
    all_to_all x1, blocking collectives, body(): lax.all_to_all(reply.reshape(devices, 2 * batches, 1, LANES), ('gx', 'gy'...  10.3 us
    pallas_call x1, Pallas kernels, body(): pl.pallas_call(functools.partial(owner_kernel, devices, per_peer, batches...  5.17 us
    pallas_call x1, Pallas kernels, body(): pl.pallas_call(functools.partial(pack_kernel, devices), out_shape=jax.Sha...  1.51 us
    ppermute x1, waiting for transfers between devices, body(): swapped = lax.ppermute(arrived, 'gy', [(i, i ^ 1) for i in range(count_gy)])  0.92 us
  transfers between devices with their start and end apart: 1, of which 1 were waited for; matrix products, arithmetic and copies ran while one was open for 0% of the time, Pallas kernels for 2%

profile of v6, /device:TPU:0, one launch (start us, length us, event | category | flops | bytes accessed | tf_op | source)
XLA Modules:
  0.0 41.5 jit_solution(8524120876993052760)
XLA Ops:
  1.3 1.5 %pack.1 = f32[800,128]{1,0:T(8,128)S(1)} custom-call(s32[1]{0:T(128)S(6)} %copy.12.load_ref, s32[4]{0:T(128)} %count_hbm.1, s32[4,32]{1,0:T(4,128)} %label_hbm.1, s32[8,128]{1,0:T(8,128)} %bitcast.19, f32[3,1024]{1,0:T(4,128)} %atom_hbm.1, s32[4,32,256]{2,1,0:T(8,128)} %shell_hbm.1, f32[3,4,256]{2,1,0:T(4,128)} %bitcast.18, f32[4,256]{1,0:T(4,128)} %charge_hbm.1), custom_call_target="tpu_custom_call" | custom-call | tf_op jit(solution)/shard_map/pack/pallas_call | solution.py:424
  2.8 20.9 %all_to_all.10 = f32[32,25,1,128]{3,2,1,0:T(1,128)S(1)} all-to-all(f32[32,25,1,128]{3,2,1,0:T(1,128)S(1)} %bitcast.16), channel_id=1, replica_groups=mesh['gx'=4,'gy'=8] {'gx','gy'}, dimensions={0} | all-to-all | bytes 819200 | tf_op jit(solution)/shard_map/all_to_all | solution.py:456
  23.7 0.1 collective-permute-start
  23.8 0.7 %own.1 = (f32[7232,128]{1,0:T(8,128)S(1)}, f32[128,128]{1,0:T(8,128)S(1)}, s32[32,128]{1,0:T(8,128)S(1)}) custom-call(f32[800,128]{1,0:T(8,128)S(1)} %bitcast.14), custom_call_target="tpu_custom_call" | custom-call | flops 2000000000 | bytes 1000 | tf_op jit(solution)/shard_map/own/pallas_call | solution.py:462
  24.5 0.9 %collective-permute-done.other_ref = f32[800,128]{1,0:T(8,128)S(1)} collective-permute-done((f32[800,128]{1,0:T(8,128)S(1)}, f32[800,128]{1,0:T(8,128)S(1)}, u32[]{:S(2)}, u32[]{:S(2)}) %collective-permute-start) | collective-permute-done | bytes 409632 | tf_op jit(solution)/shard_map/ppermute | solution.py:459
  25.5 5.2 %owner.1 = (f32[32,3136]{1,0:T(8,128)}, f32[256,128]{1,0:T(8,128)S(1)}) custom-call(s32[1]{0:T(128)} %bitcast.parity_ref, f32[800,128]{1,0:T(8,128)S(1)} %bitcast.15, f32[800,128]{1,0:T(8,128)S(1)} %collective-permute-done.other_ref, f32[7232,128]{1,0:T(8,128)S(1)} %get-tuple-element.7.y_own, f32[128,128]{1,0:T(8,128)S(1)} %get-tuple-element.8.w_own, ...), custom_call_target="tpu_custom_call" | custom-call | tf_op jit(solution)/shard_map/owner/pallas_call | solution.py:475
  30.6 10.3 %all_to_all.11 = f32[32,8,1,128]{3,1,2,0:T(8,128)S(1)} all-to-all(f32[32,8,1,128]{3,1,2,0:T(8,128)S(1)} %bitcast.17), channel_id=1, replica_groups=mesh['gx'=4,'gy'=8] {'gx','gy'}, dimensions={0} | all-to-all | bytes 262144 | tf_op jit(solution)/shard_map/all_to_all | solution.py:499
  40.9 0.6 %reduce_sum.9 = f32[8,128]{1,0:T(8,128)} reduce(f32[32,8,1,128]{3,1,2,0:T(8,128)S(1)} %all_to_all.11, f32[]{:T(128)} %constant.18.clone.1), dimensions={0,2}, to_apply=%region_0.1 | reduce | flops 31744 | bytes 135172 | tf_op jit(solution)/shard_map/reduce_sum | solution.py:502
Async XLA Ops:
  23.7 1.7 %collective-permute-start = (f32[800,128]{1,0:T(8,128)S(1)}, f32[800,128]{1,0:T(8,128)S(1)}, u32[]{:S(2)}, u32[]{:S(2)}) collective-permute-start(f32[800,128]{1,0:T(8,128)S(1)} %bitcast.13), channel_id=1, source_target_pairs={{0,1},{1,0},{2,3},{3,2},{4,5},{5,4},{6,7},{7,6},{8,9},{9,8},{10,11... | collective-permute-start | bytes 1228808 | tf_op jit(solution)/shard_map/ppermute | solution.py:459
